TPU v7x, 256 devices: a whole 4x4x8 slice. The times are simulated.
256 devices in a mesh: seq: 64 (over x, z, core), head: 4 (over y).
Axes of the slice: x: 4, y: 4, z: 8, core: 2. Of those that a mesh axis runs over, the one named last changes fastest.
Arguments:
- hidden_in: bfloat16 [256, 4096], P(None, 'seq'), may hold values from -6 to 6
- norm_gain: bfloat16 [1, 4096], P(None, 'seq'), may hold values from 0.25 to 1.75
- w_query: bfloat16 [4096, 4096], P('seq', 'head'), may hold values from -1 to 1
- w_key: bfloat16 [4096, 1024], P('seq', 'head'), may hold values from -1 to 1
- w_value: bfloat16 [4096, 1024], P('seq', 'head'), may hold values from -0.09375 to 0.09375
- w_out: bfloat16 [4096, 4096], P('head', 'seq'), may hold values from -0.09375 to 0.09375
- cache_keys: bfloat16 [262144, 8, 128], P('seq', 'head'), may hold values from -400 to 400
- cache_values: bfloat16 [262144, 8, 128], P('seq', 'head'), may hold values from -12 to 12
- lengths: int32 [64], replicated, may hold values from 512 to 4096, as said below
- span_start: int32 [1], replicated, may hold values from 0 to 256
Outputs:
- attn_out: bfloat16 [256, 4096], P('head', 'seq')
Inputs may be any that keep to these rules, and one draw needn't show every extreme that they name: Slots 0 to lengths[s] - 1 of shard s are live, the others empty; in every draw some shard is full.
All inputs are finite; a program needn't handle non-finite values.
Results may differ from a plain program's by a relative error of at most 0.039.
The roundings to bfloat16 on the way count: a program that leaves them out, or rounds other values in their place, can miss the bound.
Values may be sent and summed in bfloat16 or wider, within the bound.
A program may use at most 64 MiB of HBM per device.

v0:
```python
import math

import jax
import jax.numpy as jnp
from jax import lax
from jax.sharding import Mesh
from jax.sharding import PartitionSpec as P

D = 4096
SEQ = ("seq_0", "seq_1", "seq_2")


rope_base = 500000.0
stretch = 64.0
initial_context = 8192.0
ramp_low = 1.0
ramp_high = 32.0
epsilon = 1e-05
negative = -1e30


def sent_to_all(array, axis):
    copies = jnp.broadcast_to(array, (lax.axis_size(axis), *array.shape))
    return lax.all_to_all(copies, axis, split_axis=0, concat_axis=0, tiled=True)


def of_everyone(array, axis):
    return sent_to_all(array, axis).sum(axis=0)


def rows_for(lines, size):
    spare = -len(lines) % size
    return jnp.pad(lines, [(0, spare)] + [(0, 0)] * (lines.ndim - 1))


def laid_out(blocks, dim):
    blocks = jnp.moveaxis(blocks, 0, dim)
    dims = blocks.shape
    return blocks.reshape(*dims[:dim], dims[dim] * dims[dim + 1], *dims[dim + 2 :])


def gather_axes(array, axes, dim):
    far, near = axes
    leading = sent_to_all(array, far)
    blocks = jnp.swapaxes(sent_to_all(leading, near), 0, 1)
    return laid_out(blocks.reshape(-1, *array.shape), dim)


def cut_along(array, dim, size):
    before, after = (array.shape[:dim], array.shape[dim + 1 :])
    return jnp.moveaxis(array.reshape(*before, size, -1, *after), dim, 0)


def sent_and_summed(array, axis, dim):
    blocks = cut_along(array, dim, lax.axis_size(axis))
    arrived = lax.all_to_all(blocks, axis, split_axis=0, concat_axis=0, tiled=True)
    return arrived.sum(axis=0)


def sum_by_axis(array, axes, dim):
    far, near = axes
    own = sent_and_summed(cut_along(array, dim, lax.axis_size(far)), near, dim + 1)
    return jnp.sum(lax.all_to_all(own, far, 0, 0, tiled=True), axis=0)


def total_of(array, axes):
    lines = array.reshape(-1, array.shape[-1])
    padded = rows_for(lines, lax.axis_size(axes[0]) * lax.axis_size(axes[1]))
    whole = gather_axes(sum_by_axis(padded, axes, 0), axes, 0)
    return lax.slice_in_dim(whole, 0, len(lines)).reshape(array.shape)


def taken_together(array, axis):
    everything = sent_to_all(array, axis)
    return jnp.max(everything, axis=0)


def nested_sum(array, axes):
    padded = rows_for(array, lax.axis_size(axes[0]) * lax.axis_size(axes[1]))
    whole = gather_axes(sum_by_axis(padded, axes, 0), axes, 0)
    return lax.slice_in_dim(whole, 0, len(array)).reshape(array.shape)


def in_one(arrays, axis):
    line, at, gathered = (jnp.concatenate([a.reshape(-1) for a in arrays]), 0, [])
    running = nested_sum(line, axis)
    for a in arrays:
        gathered.append(running[at : at + a.size].reshape(a.shape))
        at += a.size
    return tuple(gathered)


def sum_at_owner(array, axis, dim):
    blocks = cut_along(array, dim, lax.axis_size(axis))
    arrived = lax.all_to_all(blocks, axis, split_axis=0, concat_axis=0, tiled=True)
    return arrived.astype(jnp.float32).sum(axis=0)


def rope_parts(positions, head_dim):
    half_dim = head_dim // 2
    indices = jnp.arange(half_dim, dtype=jnp.float32)
    base_freq = jnp.power(jnp.float32(rope_base), -2.0 * indices / head_dim)
    wavelength = 2.0 * math.pi / base_freq
    turn_count = initial_context / wavelength
    ramp_share = jnp.clip((turn_count - ramp_low) / (ramp_high - ramp_low), 0.0, 1.0)
    frequency = (1.0 - ramp_share) * base_freq / stretch + ramp_share * base_freq
    angles = positions[:, None] * frequency[None, :]
    mscale = 0.1 * math.log(stretch) + 1.0
    return (jnp.cos(angles) * mscale, jnp.sin(angles) * mscale)


def rotate(vectors, cosine, sine_part):
    half_dim = vectors.shape[-1] // 2
    lower_half = vectors[..., :half_dim]
    upper_half = vectors[..., half_dim:]
    cosine = cosine[:, None, :]
    sine_part = sine_part[:, None, :]
    return jnp.concatenate(
        [
            lower_half * cosine - upper_half * sine_part,
            upper_half * cosine + lower_half * sine_part,
        ],
        -1,
    )


def round_trip(values):
    return lax.optimization_barrier(values.astype(jnp.bfloat16)).astype(jnp.float32)


def attend(running, queries, key_block, value_block, visible):
    maxima, totals, weighted = running
    scores = jnp.einsum("tgrd,kgd->grtk", queries, key_block, preferred_element_type=jnp.float32)
    scores = jnp.where(visible, scores, negative)
    new_max = jnp.maximum(maxima, jnp.max(scores, axis=-1))
    probability = jnp.where(visible, jnp.exp(scores - new_max[..., None]), 0.0)
    rescale = jnp.exp(maxima - new_max)
    totals = totals * rescale + jnp.sum(probability, axis=-1)
    weighted = weighted * rescale[..., None] + jnp.einsum(
        "grtk,kgd->grtd",
        probability.astype(jnp.bfloat16),
        value_block,
        preferred_element_type=jnp.float32,
    )
    return (new_max, totals, weighted)


def local(
    hidden_in,
    norm_gain,
    w_query,
    w_key,
    w_value,
    w_out,
    cache_keys,
    cache_values,
    lengths,
    span_start,
):
    seq_count = lax.axis_size(SEQ)
    my_index = lax.axis_index(SEQ)
    span_len = hidden_in.shape[0]
    local_kv = cache_keys.shape[1]
    head_dim = cache_keys.shape[2]
    group_size = w_query.shape[1] // (local_kv * head_dim)
    kv_cols = w_key.shape[1]
    row_count = span_len // seq_count
    first_new = my_index * row_count
    input_f32 = hidden_in.astype(jnp.float32)
    square_sums = of_everyone(jnp.sum(input_f32 * input_f32, axis=1), SEQ)
    inv_rms = lax.rsqrt(square_sums[:, None] / D + epsilon)
    normed = (input_f32 * inv_rms * norm_gain.astype(jnp.float32)).astype(jnp.bfloat16)
    queries = total_of(
        jnp.dot(normed, w_query, preferred_element_type=jnp.float32), (("seq_0", "seq_1"), "seq_2")
    )
    kv_own = sent_and_summed(
        jnp.concatenate(
            [
                jnp.dot(normed, w_key, preferred_element_type=jnp.float32),
                jnp.dot(normed, w_value, preferred_element_type=jnp.float32),
            ],
            1,
        ),
        SEQ,
        0,
    )
    key_own = kv_own[:, :kv_cols]
    value_own = kv_own[:, kv_cols:]
    shard_ids = jnp.arange(lengths.shape[0], dtype=jnp.int32)
    offset = jnp.sum(jnp.where(shard_ids < my_index, lengths, 0))
    live_count = jnp.sum(jnp.where(shard_ids == my_index, lengths, 0))
    first_pos = jnp.sum(lengths) + span_start[0]
    query_pos = (first_pos + jnp.arange(span_len, dtype=jnp.int32)).astype(jnp.float32)
    cosine, sine_part = rope_parts(query_pos, head_dim)
    rotated = rotate(
        queries.reshape(span_len, local_kv * group_size, head_dim), cosine, sine_part
    ) * head_dim ** (-0.5)
    query_low = rotated.astype(jnp.bfloat16).reshape(span_len, local_kv, group_size, head_dim)
    my_keys = round_trip(key_own).reshape(row_count, local_kv, head_dim)
    my_values = value_own.astype(jnp.bfloat16).reshape(row_count, local_kv, head_dim)
    new_pos = (first_pos + first_new + jnp.arange(row_count, dtype=jnp.int32)).astype(jnp.float32)
    new_cos, new_sin = rope_parts(new_pos, head_dim)
    new_key_rot = rotate(my_keys, new_cos, new_sin).astype(jnp.bfloat16)
    block_len = math.gcd(cache_keys.shape[0], 1024)

    def sweep_block(block_index, running):
        block_start = block_index * block_len
        key_block = lax.dynamic_slice_in_dim(cache_keys, block_start, block_len, 0).astype(
            jnp.float32
        )
        value_block = lax.dynamic_slice_in_dim(cache_values, block_start, block_len, 0)
        slot_ids = block_start + jnp.arange(block_len, dtype=jnp.int32)
        occupied = slot_ids < live_count
        positions = (offset + slot_ids).astype(jnp.float32)
        block_cos, block_sin = rope_parts(positions, head_dim)
        block_keys = rotate(key_block, block_cos, block_sin).astype(jnp.bfloat16)
        return attend(running, query_low, block_keys, value_block, occupied[None, None, None, :])

    running = (
        jnp.full((local_kv, group_size, span_len), negative, jnp.float32),
        jnp.zeros((local_kv, group_size, span_len), jnp.float32),
        jnp.zeros((local_kv, group_size, span_len, head_dim), jnp.float32),
    )
    block_total = (live_count + block_len - 1) // block_len
    running = lax.fori_loop(0, block_total, sweep_block, running)
    query_rows = jnp.arange(span_len, dtype=jnp.int32)[:, None]
    key_rows = first_new + jnp.arange(row_count, dtype=jnp.int32)[None, :]
    maxima, totals, weighted = attend(
        running, query_low, new_key_rot, my_values, (key_rows <= query_rows)[None, None]
    )
    global_max = taken_together(maxima, SEQ)
    rescale = jnp.exp(maxima - global_max)
    totals, weighted = in_one(
        (totals * rescale, weighted * rescale[..., None]), (("seq_0", "seq_1"), "seq_2")
    )
    attended = (
        (weighted / totals[..., None])
        .transpose(2, 0, 1, 3)
        .reshape(span_len, local_kv * group_size * head_dim)
    )
    attended = attended.astype(jnp.bfloat16)
    partial_out = jnp.dot(attended, w_out, preferred_element_type=jnp.float32)
    return sum_at_owner(partial_out.astype(jnp.bfloat16), "head", 0).astype(jnp.bfloat16)


def solution(mesh):
    finer = Mesh(
        mesh.devices.reshape(4, 8, 2, mesh.shape["head"]), ("seq_0", "seq_1", "seq_2", "head")
    )
    return jax.shard_map(
        local,
        mesh=finer,
        in_specs=(
            P(None, SEQ),
            P(None, SEQ),
            P(SEQ, "head"),
            P(SEQ, "head"),
            P(SEQ, "head"),
            P("head", SEQ),
            P(SEQ, "head", None),
            P(SEQ, "head", None),
            P(),
            P(),
        ),
        out_specs=P("head", SEQ),
        check_vma=False,
    )
```

profile of v0, /device:TPU:1, one launch (start us, length us, event | category | flops | bytes accessed | tf_op | source)
XLA Modules:
  0.0 251.7 jit_solution(4500238396487724412)
XLA Ops:
  0.0 0.8 fusion.26
  0.8 0.7 broadcast_in_dim.106
  1.5 13.0 %all-to-all-start = ((f32[64,1,256]{2,1,0:T(1,128)}), f32[64,1,256]{2,1,0:T(1,128)S(1)}, u32[]{:S(2)}, u32[]{:S(2)}) async-start(f32[64,1,256]{2,1,0:T(1,128)} %broadcast_in_dim.106), calls=%async_computation | async-start | bytes 131072 | tf_op jit(solution)/shard_map/all_to_all | solution.py:24
  14.5 0.7 bitcast_convert_fusion.1
  15.1 9.1 %all-to-all-done = f32[64,1,256]{2,1,0:T(1,128)S(1)} async-done(((f32[64,1,256]{2,1,0:T(1,128)}), f32[64,1,256]{2,1,0:T(1,128)S(1)}, u32[]{:S(2)}, u32[]{:S(2)}) %all-to-all-start) | async-done | bytes 65568 | tf_op jit(solution)/shard_map/all_to_all | solution.py:24
  24.3 1.1 fusion.47
  25.5 0.3 reshape_reshape.9
  25.9 4.6 %all_to_all.69 = f32[2,32,4,1024]{3,2,1,0:T(4,128)S(1)} all-to-all(f32[2,32,4,1024]{3,2,1,0:T(4,128)S(1)} %bitcast.123), channel_id=1, replica_groups=mesh['seq_0'=4,'seq_1'=8,'seq_2'=2,'head'=4] {'seq_2'}, dimensions={0} | all-to-all | bytes 2097152 | tf_op jit(solution)/shard_map/all_to_all | solution.py:56
  30.5 1.2 reduce_sum.127
  31.8 3.9 %all-to-all-start.2 = ((f32[32,4,1024]{2,1,0:T(4,128)}), f32[32,4,1024]{2,1,0:T(4,128)S(1)}, u32[]{:S(2)}, u32[]{:S(2)}) async-start(f32[32,4,1024]{2,1,0:T(4,128)} %reduce_sum.127), calls=%async_computation.2 | async-start | bytes 1048576 | tf_op jit(solution)/shard_map/all_to_all | solution.py:63
  35.7 0.2 fusion.43
  36.0 0.2 fusion.45
  36.3 0.2 copy.80
  36.5 0.9 reshape.285
  37.4 13.2 %all-to-all-done.2 = f32[32,4,1024]{2,1,0:T(4,128)S(1)} async-done(((f32[32,4,1024]{2,1,0:T(4,128)}), f32[32,4,1024]{2,1,0:T(4,128)S(1)}, u32[]{:S(2)}, u32[]{:S(2)}) %all-to-all-start.2) | async-done | bytes 524320 | tf_op jit(solution)/shard_map/all_to_all | solution.py:63
  50.6 8.7 %all-to-all-start.5 = ((f32[64,4,512]{2,1,0:T(4,128)}), f32[64,4,512]{2,1,0:T(4,128)S(1)}, u32[]{:S(2)}, u32[]{:S(2)}) async-start(f32[64,4,512]{2,1,0:T(4,128)} %reshape.285), calls=%async_computation.5 | async-start | bytes 1048576 | tf_op jit(solution)/shard_map/all_to_all | solution.py:56
  59.3 0.7 fusion.49
  62.2 14.3 %all-to-all-done.5 = f32[64,4,512]{2,1,0:T(4,128)S(1)} async-done(((f32[64,4,512]{2,1,0:T(4,128)}), f32[64,4,512]{2,1,0:T(4,128)S(1)}, u32[]{:S(2)}, u32[]{:S(2)}) %all-to-all-start.5) | async-done | bytes 524320 | tf_op jit(solution)/shard_map/all_to_all | solution.py:56
  76.6 0.9 broadcast_in_dim.107
  77.5 5.2 %all-to-all-start.3 = ((f32[32,4,1024]{2,1,0:T(4,128)}), f32[32,4,1024]{2,1,0:T(4,128)S(1)}, u32[]{:S(2)}, u32[]{:S(2)}) async-start(f32[32,4,1024]{2,1,0:T(4,128)} %broadcast_in_dim.107), calls=%async_computation.3 | async-start | bytes 1048576 | tf_op jit(solution)/shard_map/all_to_all | solution.py:24
  82.7 0.1 fusion.35
  82.8 0.5 fusion.24
  83.3 0.1 reduce_sum.130
  83.5 13.6 %all-to-all-done.3 = f32[32,4,1024]{2,1,0:T(4,128)S(1)} async-done(((f32[32,4,1024]{2,1,0:T(4,128)}), f32[32,4,1024]{2,1,0:T(4,128)S(1)}, u32[]{:S(2)}, u32[]{:S(2)}) %all-to-all-start.3) | async-done | bytes 524320 | tf_op jit(solution)/shard_map/all_to_all | solution.py:24
  97.1 0.3 broadcast_in_dim.108
  97.4 7.4 %all_to_all.70 = f32[2,32,4,1024]{3,2,1,0:T(4,128)S(1)} all-to-all(f32[2,32,4,1024]{3,2,1,0:T(4,128)S(1)} %broadcast_in_dim.108), channel_id=1, replica_groups=mesh['seq_0'=4,'seq_1'=8,'seq_2'=2,'head'=4] {'seq_2'}, dimensions={0} | all-to-all | bytes 2097152 | tf_op jit(solution)/shard_map/all_to_all | solution.py:24
  104.9 0.4 reshape_reshape_reshape.3
  105.3 0.5 multiply_subtract_fusion
  105.8 0.2 copy.77
  106.0 0.2 copy.76
  106.2 0.3 fusion.22
  106.7 12.4 %while.16 = (s32[]{:T(128)}, f32[2,4,256]{2,1,0:T(4,128)S(1)}, f32[2,4,256]{2,1,0:T(4,128)S(1)}, f32[2,4,256,128]{3,2,1,0:T(8,128)S(1)}, s32[]{:T(128)}, /*index...) while((s32[]{:T(128)}, f32[2,4,256]{2,1,0:T(4,128)S(1)}, ...), condition=%wide.region_10.11_spmd, body=%wide.region_7.0_spmd.sunk | while | flops 1097803520 | bytes 35271368 | solution.py:225
  106.9 1.9 constant_dynamic-slice_fusion.3
  108.9 0.6 add_convert_fusion.6
  109.5 1.9 fusion.67
  111.4 0.5 subtract_convert_fusion.3
  111.9 0.7 fusion.66
  112.6 1.4 bitcast_reduce_fusion.3
  114.0 2.1 fusion.68
  116.1 2.9 %fusion.69 = f32[2,4,256,128]{3,2,1,0:T(8,128)S(1)} fusion(f32[2,1024,256,4]{2,1,3,0:T(8,128)S(1)} %get-tuple-element.337, f32[2,4,256]{2,1,0:T(4,128)S(1)} %max.30, pred[1024]{0:T(1024)(128)(4,1)S(1)} %fusion.66, f32[2,4,256,128]{3,2,1,0:T(8,128)S(1)} %get-tuple-element.358, bf16[1024,2,128]{2,1,0:T(2,128)(2,1)S(1)} %get-tuple-element.340, ...), kind=kOutput, calls=%fused_computation.9.clone.1 | convolution fusion | flops 545783808 | bytes 11027456 | tf_op jit(solution)/shard_map/while/body/grtk,kgd->grtd/dot_general | solution.py:139
  119.1 0.3 fusion.50
  119.4 0.9 broadcast_in_dim.112
  120.3 42.9 %all-to-all-start.6 = ((f32[64,2,4,256]{3,2,1,0:T(4,128)}), f32[64,2,4,256]{3,2,1,0:T(4,128)S(1)}, u32[]{:S(2)}, u32[]{:S(2)}) async-start(f32[64,2,4,256]{3,2,1,0:T(4,128)} %broadcast_in_dim.112), calls=%async_computation.6 | async-start | bytes 1048576 | tf_op jit(solution)/shard_map/all_to_all | solution.py:24
  163.2 17.2 %all-to-all-done.6 = f32[64,2,4,256]{3,2,1,0:T(4,128)S(1)} async-done(((f32[64,2,4,256]{3,2,1,0:T(4,128)}), f32[64,2,4,256]{3,2,1,0:T(4,128)S(1)}, u32[]{:S(2)}, u32[]{:S(2)}) %all-to-all-start.6) | async-done | bytes 524320 | tf_op jit(solution)/shard_map/all_to_all | solution.py:24
  180.5 0.1 reduce_max.31
  180.6 0.9 fusion.20
  181.6 1.0 reshape_reshape.10
  182.7 4.5 %all_to_all.71 = f32[2,32,4128]{2,1,0:T(8,128)S(1)} all-to-all(f32[2,32,4128]{2,1,0:T(8,128)S(1)} %copy.82), channel_id=1, replica_groups=mesh['seq_0'=4,'seq_1'=8,'seq_2'=2,'head'=4] {'seq_2'}, dimensions={0} | all-to-all | bytes 2113536 | tf_op jit(solution)/shard_map/all_to_all | solution.py:56
  187.3 0.4 all_to_all.51
  187.7 19.8 %all_to_all.72 = f32[32,1,4128]{2,1,0:T(1,128)S(1)} all-to-all(f32[32,1,4128]{2,1,0:T(1,128)S(1)} %all_to_all.51), channel_id=1, replica_groups=mesh['seq_0'=4,'seq_1'=8,'seq_2'=2,'head'=4] {'seq_0','seq_1'}, dimensions={0} | all-to-all | bytes 1056768 | tf_op jit(solution)/shard_map/all_to_all | solution.py:63
  207.5 0.3 reduce_sum.133
  207.8 0.3 broadcast_in_dim.113
  208.1 23.1 %all_to_all.73 = f32[32,1,4128]{2,1,0:T(1,128)S(1)} all-to-all(f32[32,1,4128]{2,1,0:T(1,128)S(1)} %broadcast_in_dim.113), channel_id=1, replica_groups=mesh['seq_0'=4,'seq_1'=8,'seq_2'=2,'head'=4] {'seq_0','seq_1'}, dimensions={0} | all-to-all | bytes 1056768 | tf_op jit(solution)/shard_map/all_to_all | solution.py:24
  231.3 7.2 %all_to_all.74 = f32[2,32,4128]{2,1,0:T(8,128)S(1)} all-to-all(f32[2,32,4128]{2,1,0:T(8,128)S(1)} %broadcast_in_dim.114), channel_id=1, replica_groups=mesh['seq_0'=4,'seq_1'=8,'seq_2'=2,'head'=4] {'seq_2'}, dimensions={0} | all-to-all | bytes 2113536 | tf_op jit(solution)/shard_map/all_to_all | solution.py:24
  238.4 0.8 copy.83
  239.3 0.9 reshape_reshape.11
  240.1 1.3 slice.48
  241.5 0.3 fusion.23
  241.9 0.2 copy.85
  242.1 0.2 convolution_convert_fusion
  242.5 0.1 reshape.300
  242.6 8.3 %all_to_all.75 = bf16[4,2,2048]{2,1,0:T(2,128)(2,1)S(1)} all-to-all(bf16[4,2,2048]{2,1,0:T(2,128)(2,1)S(1)} %reshape.300), channel_id=1, replica_groups=mesh['seq_0'=4,'seq_1'=8,'seq_2'=2,'head'=4] {'head'}, dimensions={0} | all-to-all | bytes 65536 | tf_op jit(solution)/shard_map/all_to_all | solution.py:95
  250.9 0.1 reshape.301
  251.0 0.7 copy.88
  (48 shorter events, 1.4 us)
Async XLA Ops:
  0.0 24.3 %copy-start = (bf16[64,1024]{1,0:T(8,128)(2,1)S(1)}, bf16[64,1024]{1,0:T(8,128)(2,1)}, u32[]{:S(2)}) copy-start(bf16[64,1024]{1,0:T(8,128)(2,1)} %param.14) | copy-start | bytes 393220
  1.5 22.8 %all-to-all-start = ((f32[64,1,256]{2,1,0:T(1,128)}), f32[64,1,256]{2,1,0:T(1,128)S(1)}, u32[]{:S(2)}, u32[]{:S(2)}) async-start(f32[64,1,256]{2,1,0:T(1,128)} %broadcast_in_dim.106), calls=%async_computation | async-start | bytes 131072 | tf_op jit(solution)/shard_map/all_to_all | solution.py:24
  25.5 10.2 %copy-start.1 = (bf16[256,64]{0,1:T(8,128)(2,1)S(1)}, bf16[256,64]{0,1:T(8,128)(2,1)}, u32[]{:S(2)}) copy-start(bf16[256,64]{0,1:T(8,128)(2,1)} %param.12) | copy-start | bytes 98308
  25.5 10.2 %copy-start.3 = (bf16[64,256]{1,0:T(8,128)(2,1)S(1)}, bf16[64,256]{1,0:T(8,128)(2,1)}, u32[]{:S(2)}) copy-start(bf16[64,256]{1,0:T(8,128)(2,1)} %param.16) | copy-start | bytes 98308
  25.5 10.4 %copy-start.4 = (bf16[64,256]{1,0:T(8,128)(2,1)S(1)}, bf16[64,256]{1,0:T(8,128)(2,1)}, u32[]{:S(2)}) copy-start(bf16[64,256]{1,0:T(8,128)(2,1)} %param.15) | copy-start | bytes 98308
  30.5 28.8 %copy-start.5 = (s32[64]{0:T(128)S(1)}, s32[64]{0:T(128)}, u32[]{:S(2)}) copy-start(s32[64]{0:T(128)} %param.20) | copy-start | bytes 772
  31.8 18.8 %all-to-all-start.2 = ((f32[32,4,1024]{2,1,0:T(4,128)}), f32[32,4,1024]{2,1,0:T(4,128)S(1)}, u32[]{:S(2)}, u32[]{:S(2)}) async-start(f32[32,4,1024]{2,1,0:T(4,128)} %reduce_sum.127), calls=%async_computation.2 | async-start | bytes 1048576 | tf_op jit(solution)/shard_map/all_to_all | solution.py:63
  50.6 26.0 %all-to-all-start.5 = ((f32[64,4,512]{2,1,0:T(4,128)}), f32[64,4,512]{2,1,0:T(4,128)S(1)}, u32[]{:S(2)}, u32[]{:S(2)}) async-start(f32[64,4,512]{2,1,0:T(4,128)} %reshape.285), calls=%async_computation.5 | async-start | bytes 1048576 | tf_op jit(solution)/shard_map/all_to_all | solution.py:56
  77.5 19.7 %all-to-all-start.3 = ((f32[32,4,1024]{2,1,0:T(4,128)}), f32[32,4,1024]{2,1,0:T(4,128)S(1)}, u32[]{:S(2)}, u32[]{:S(2)}) async-start(f32[32,4,1024]{2,1,0:T(4,128)} %broadcast_in_dim.107), calls=%async_computation.3 | async-start | bytes 1048576 | tf_op jit(solution)/shard_map/all_to_all | solution.py:24
  120.3 60.2 %all-to-all-start.6 = ((f32[64,2,4,256]{3,2,1,0:T(4,128)}), f32[64,2,4,256]{3,2,1,0:T(4,128)S(1)}, u32[]{:S(2)}, u32[]{:S(2)}) async-start(f32[64,2,4,256]{3,2,1,0:T(4,128)} %broadcast_in_dim.112), calls=%async_computation.6 | async-start | bytes 1048576 | tf_op jit(solution)/shard_map/all_to_all | solution.py:24
  239.3 2.8 %copy-start.2 = (bf16[1024,64]{0,1:T(8,128)(2,1)S(1)}, bf16[1024,64]{0,1:T(8,128)(2,1)}, u32[]{:S(2)}) copy-start(bf16[1024,64]{0,1:T(8,128)(2,1)} %param.17) | copy-start | bytes 393220
where the time goes:
time: 254 us; the launch traced here: 252 us
  blocking collectives  74.8 us (29%)
  starting transfers between devices  73.7 us (29%)
  waiting for transfers between devices  67.4 us (27%)
  local copies, waits for them, and re-layouts  13.3 us (5%)
  other arithmetic  12.4 us (5%)
  matrix products  7.33 us (3%)
    all_to_all x3, starting transfers between devices, sent_to_all(): return lax.all_to_all(copies, axis, split_axis=0, concat_axis=0, tiled=True)  61.1 us
    all_to_all x3, waiting for transfers between devices, sent_to_all(): return lax.all_to_all(copies, axis, split_axis=0, concat_axis=0, tiled=True)  40 us
    all_to_all x3, blocking collectives, sent_to_all(): return lax.all_to_all(copies, axis, split_axis=0, concat_axis=0, tiled=True)  37.6 us
    all_to_all x1, blocking collectives, sum_by_axis(): return jnp.sum(lax.all_to_all(own, far, 0, 0, tiled=True), axis=0)  19.8 us
    all_to_all x1, waiting for transfers between devices, sent_and_summed(): lax.all_to_all(blocks, axis, split_axis=0, concat_axis=0, tiled=True)  14.3 us
    all_to_all x1, waiting for transfers between devices, sum_by_axis(): return jnp.sum(lax.all_to_all(own, far, 0, 0, tiled=True), axis=0)  13.2 us
    all_to_all x2, blocking collectives, sent_and_summed(): lax.all_to_all(blocks, axis, split_axis=0, concat_axis=0, tiled=True)  9.12 us
    all_to_all x1, starting transfers between devices, sent_and_summed(): lax.all_to_all(blocks, axis, split_axis=0, concat_axis=0, tiled=True)  8.71 us
  transfers between devices with their start and end apart: 5, of which 5 were waited for; matrix products, arithmetic and copies ran while one was open for 2% of the time, Pallas kernels for 0%

commit v1 on v0

v1 whole, which is shorter than its diff:
```python
import functools
import math

import jax
import jax.numpy as jnp
from jax import lax
from jax.experimental import pallas as pl
from jax.experimental.pallas import tpu as pltpu
from jax.sharding import Mesh
from jax.sharding import PartitionSpec as P

F32 = jnp.float32
BF16 = jnp.bfloat16
MESH = pl.DeviceIdType.MESH
LANES = 128
HALF = 64
ROWS = 32
CHUNK = 128
KEYS = 512

rope_base = 500000.0
stretch = 64.0
initial_context = 8192.0
ramp_low = 1.0
ramp_high = 32.0
epsilon = 1e-05
negative = -1e30
mscale = 0.1 * math.log(stretch) + 1.0


def frequencies():
    indices = jnp.arange(HALF, dtype=F32)
    base = jnp.power(F32(rope_base), -2.0 * indices / LANES)
    turns = initial_context / (2.0 * math.pi / base)
    share = jnp.clip((turns - ramp_low) / (ramp_high - ramp_low), 0.0, 1.0)
    freq = (1.0 - share) * base / stretch + share * base
    return jnp.concatenate([freq, freq])[None, :]


def cos_sin(angles):
    turns = jnp.floor(angles * (1.0 / (2.0 * math.pi)) + 0.5)
    first, second = 6.28125, 253.0 / 2.0**17
    third = 2.0 * math.pi - first - second
    rest = angles - turns * first - turns * second - turns * third
    return jnp.cos(rest), jnp.sin(rest)


def iota(shape, dim):
    return lax.broadcasted_iota(jnp.int32, shape, dim)


def signed(sine):
    return jnp.where(iota(sine.shape, 1) < HALF, -sine, sine)


def rotated(vectors, cosine, sine):
    return vectors * cosine + pltpu.roll(vectors, HALF, 1) * sine


def hi_lo(sums):
    high = sums.astype(BF16).astype(F32)
    return jnp.where(iota(sums.shape, 1) < HALF, high, sums - high)


def as_columns(rows):
    spare = LANES - rows.shape[0]
    if spare:
        rows = jnp.concatenate([rows, jnp.zeros((spare, LANES), F32)], 0)
    return rows.T


def kernel(
    dims,
    h_ref, g_ref, wq_ref, wk_ref, wv_ref, wo_ref, freq_ref, len_ref, start_ref, k_hbm, v_hbm,
    out_ref,
    kraw, vraw, tmp, ks, vs, tab_a, tab_b, k0,
    sb, rb, own, xs, xr, zs, zr, inv_ref, qbuf, s_ref,
    ob, lb, obs, obr, lss, lsr, oxs, oxr, lxs, lxr, ozs, ozr, lzs, lzr, wt,
    att, wobuf, p5s, p5r,
    kv_sem,
    c1s, c1r, x1s, x1r, z1s, z1r,
    z2s, z2r, x2s, x2r, c2s, c2r, ws, wr,
    c3s, c3r, c3ls, c3lr, x3s, x3r, x3ls, x3lr, z3s, z3r, z3ls, z3lr,
    z4s, z4r, c4s, c4r, y5s, y5r,
):
    nx, nz, nc, ny, d_model = dims
    x, z, c, y = (lax.axis_index(n) for n in ("x", "z", "c", "y"))
    sib = 1 - c
    slots = kraw.shape[0] // 2
    group = wq_ref.shape[1] // wk_ref.shape[1]
    kv = wk_ref.shape[1] // LANES
    heads = kv * group
    quarters = nz // kv
    tail = ROWS // quarters
    qc = heads * LANES
    kc = kv * LANES
    per_x = nc * ROWS

    def copy(src, dst, send, recv, **to):
        return pltpu.make_async_remote_copy(
            src_ref=src, dst_ref=dst, send_sem=send, recv_sem=recv, device_id=to, device_id_type=MESH
        )

    def other_x(k):
        return lax.rem(x + k, nx)

    def other_z(k):
        return lax.rem(z + k, nz)

    x_far = sorted(range(1, nx), key=lambda k: -min(k, nx - k))
    z_far = sorted(range(1, nz), key=lambda k: -min(k, nz - k))
    z_near = z_far[::-1]
    x_near = x_far[::-1]

    get_k = pltpu.make_async_copy(k_hbm, kraw, kv_sem.at[0])
    get_v = pltpu.make_async_copy(v_hbm, vraw, kv_sem.at[1])
    get_k.start()
    get_v.start()

    barrier = pltpu.get_barrier_semaphore()

    def greet(**to):
        pl.semaphore_signal(barrier, inc=1, device_id=to, device_id_type=MESH)

    greet(c=sib)
    for k in range(1, nx):
        greet(x=other_x(k))
    for k in range(1, nz):
        greet(z=other_z(k))
    for k in range(1, ny):
        greet(x=y, y=lax.rem(y + k, ny))

    @pl.when(x != y)
    def _():
        greet(x=y, y=y)

    hidden = h_ref[...].astype(F32)
    scaled = (hidden * g_ref[...].astype(F32)).astype(BF16)
    squares = jnp.sum(hidden * hidden, axis=1, keepdims=True)
    sums = hi_lo(jnp.broadcast_to(squares, (h_ref.shape[0], LANES)))

    def part(value, cc):
        blocks = [
            jnp.where(cc == 0, value[b * per_x : b * per_x + ROWS], value[b * per_x + ROWS : b * per_x + 2 * ROWS])
            for b in range(nx)
        ]
        return jnp.concatenate(blocks, 0)

    def project(cc, store):
        rows = part(scaled.astype(F32), cc).astype(BF16)
        for at, w in ((0, wq_ref), (qc, wk_ref), (qc + kc, wv_ref)):
            got = jnp.dot(rows, w[...], preferred_element_type=F32)
            for b in range(nx):
                store(b, at, got[b * ROWS : (b + 1) * ROWS])
        extra = part(sums, cc)
        for b in range(nx):
            store(b, qc + 2 * kc, extra[b * ROWS : (b + 1) * ROWS])

    def to_sibling(b, at, value):
        sb[b, :, at : at + value.shape[1]] = value.astype(BF16)

    def to_own(b, at, value):
        own[b, :, at : at + value.shape[1]] = value

    project(sib, to_sibling)

    my = (x * nz + z) * nc + c
    count = nx * nz * nc

    def add_lengths(r, carry):
        before, total = carry
        return before + jnp.where(r < my, len_ref[r], 0), total + len_ref[r]

    offset, first_pos = lax.fori_loop(0, count, add_lengths, (jnp.int32(0), jnp.int32(0)))
    first_pos = first_pos + start_ref[0]
    live = len_ref[my]
    freq = freq_ref[...]

    peers = 1 + (nx - 1) + (nz - 1) + (ny - 1)
    pl.semaphore_wait(barrier, jnp.where(x != y, peers + 1, peers))

    core1 = [copy(sb.at[b], rb.at[b], c1s.at[b], c1r.at[b], c=sib) for b in range(nx)]
    for b in range(nx):
        core1[b].start()

    project(c, to_own)
    half = wo_ref.shape[0] // 2
    wobuf[x] = jnp.concatenate([wo_ref[0:half, :], wo_ref[half:, :]], 1)

    for b in range(nx):
        core1[b].wait_recv()
    for k in x_far:
        b = other_x(k)
        xs[b] = (own[b] + rb[b].astype(F32)).astype(BF16)
        copy(xs.at[b], xr.at[x], x1s.at[b], x1r.at[x], x=b).start()

    a_count = slots // CHUNK
    a_pos = (offset + CHUNK * iota((a_count, LANES), 0)).astype(F32)
    a_cos, a_sin = cos_sin(a_pos * freq)
    tab_a[0] = a_cos * mscale
    tab_a[1] = a_sin * mscale
    b_cos, b_sin = cos_sin(iota((CHUNK, LANES), 0).astype(F32) * freq)
    tab_b[0] = b_cos
    tab_b[1] = b_sin

    get_k.wait()

    def rotate_chunk(a, _):
        at = pl.multiple_of(a * CHUNK, CHUNK)
        tmp[...] = kraw[pl.ds(pl.multiple_of(2 * at, 2 * CHUNK), 2 * CHUNK), :].astype(F32)
        cos_a = tab_a[0, pl.ds(a, 1), :]
        sin_a = tab_a[1, pl.ds(a, 1), :]
        cosine = cos_a * tab_b[0] - sin_a * tab_b[1]
        sine = signed(sin_a * tab_b[0] + cos_a * tab_b[1])
        alive = at + iota((CHUNK, LANES), 0) < live
        for g in range(kv):
            keys = rotated(tmp[pl.ds(g, CHUNK, stride=kv), :], cosine, sine)

            @pl.when(a == 0)
            def _():
                k0[g] = keys[0:8]

            keys = jnp.where(alive, keys, k0[g, 0:1, :])
            ks[g, pl.ds(at, CHUNK), :] = keys.astype(BF16)
        return 0

    lax.fori_loop(0, a_count, rotate_chunk, 0)

    gathered = own[x] + rb[x].astype(F32)
    for k in x_near:
        b = other_x(k)
        copy(xs.at[b], xr.at[b], x1s.at[b], x1r.at[b], x=b).wait_recv()
        gathered = gathered + xr[b].astype(F32)
    own[x] = gathered
    mixed = own[x, :, qc + 2 * kc : qc + 2 * kc + LANES]
    zs_sums = hi_lo(mixed + pltpu.roll(mixed, HALF, 1)).astype(BF16)
    for t in range(nz):
        g, quarter = t // quarters, t % quarters
        zs[t, 0:ROWS, :] = own[x, :, t * LANES : (t + 1) * LANES].astype(BF16)
        pair = [
            own[x, quarter * tail : (quarter + 1) * tail, at + g * LANES : at + (g + 1) * LANES]
            for at in (qc, qc + kc)
        ]
        zs[t, ROWS : ROWS + 2 * tail, :] = jnp.concatenate(pair, 0).astype(BF16)
        zs[t, ROWS + 2 * tail :, :] = zs_sums
    for k in z_far:
        b = other_z(k)
        copy(zs.at[b], zr.at[z], z1s.at[b], z1r.at[z], z=b).start()

    get_v.wait()

    def value_chunk(a, _):
        at = pl.multiple_of(a * CHUNK, CHUNK)
        tmp[...] = vraw[pl.ds(pl.multiple_of(2 * at, 2 * CHUNK), 2 * CHUNK), :].astype(F32)
        alive = at + iota((CHUNK, LANES), 0) < live
        ones = jnp.where(alive, 1.0, 0.0).astype(BF16)
        for g in range(kv):
            values = jnp.where(alive, tmp[pl.ds(g, CHUNK, stride=kv), :], 0.0)
            vs[g, pl.ds(at, CHUNK), 0:LANES] = values.astype(BF16)
            vs[g, pl.ds(at, CHUNK), LANES:] = ones
        return 0

    lax.fori_loop(0, a_count, value_chunk, 0)

    total = zs[z].astype(F32)
    for k in z_near:
        b = other_z(k)
        copy(zs.at[b], zr.at[b], z1s.at[b], z1r.at[b], z=b).wait_recv()
        total = total + zr[b].astype(F32)
    mixed = total[ROWS + 2 * tail :]
    inverse = lax.rsqrt((mixed + pltpu.roll(mixed, HALF, 1)) * (1.0 / d_model) + epsilon)
    inv_ref[...] = inverse
    my_g, my_quarter = lax.div(z, quarters), lax.rem(z, quarters)
    first_token = x * per_x + c * ROWS
    q_pos = (first_pos + first_token + iota((ROWS, LANES), 0)).astype(F32)
    q_cos, q_sin = cos_sin(q_pos * freq)
    scale = LANES**-0.5
    query = rotated(total[0:ROWS] * inverse, q_cos * mscale, signed(q_sin * mscale)) * scale
    qbuf[c, x, z] = query.astype(BF16)

    z2 = []
    for k in z_far:
        b = other_z(k)
        copy(qbuf.at[c, x, z], qbuf.at[c, x, z], z2s.at[b], z2r.at[z], z=b).start()

    def piece_to_x(t):
        for k in x_far:
            b = other_x(k)
            copy(qbuf.at[c, x, t], qbuf.at[c, x, t], x2s.at[b, t], x2r.at[x, t], x=b).start()

    piece_to_x(z)

    k_first = first_token + my_quarter * tail
    inv_new = inv_ref[pl.ds(pl.multiple_of(my_quarter * tail, tail), tail), :]
    k_pos = (first_pos + k_first + iota((tail, LANES), 0)).astype(F32)
    k_cos, k_sin = cos_sin(k_pos * freq)
    new_k = (total[ROWS : ROWS + tail] * inv_new).astype(BF16).astype(F32)
    new_k = rotated(new_k, k_cos * mscale, signed(k_sin * mscale))
    new_v = total[ROWS + tail : ROWS + 2 * tail] * inv_new
    empty = jnp.zeros((LANES - tail, LANES), F32)
    new_k = jnp.concatenate([new_k, empty], 0).astype(BF16)
    new_v = jnp.concatenate([new_v, empty], 0).astype(BF16)
    new_ones = jnp.where(iota((LANES, LANES), 0) < tail, 1.0, 0.0).astype(BF16)
    for g in range(kv):
        ks[g, slots:, :] = new_k
        vs[g, slots:, 0:LANES] = new_v
        vs[g, slots:, LANES:] = new_ones

    for k in z_near:
        b = other_z(k)
        copy(qbuf.at[c, x, b], qbuf.at[c, x, b], z2s.at[b], z2r.at[b], z=b).wait_recv()
        piece_to_x(b)

    def block_to_core(b):
        return copy(qbuf.at[c, b], qbuf.at[c, b], c2s.at[b], c2r.at[b], c=sib)

    block_to_core(x).start()
    for k in x_near:
        b = other_x(k)
        for t in range(nz):
            copy(qbuf.at[c, b, t], qbuf.at[c, b, t], x2s.at[b, t], x2r.at[b, t], x=b).wait_recv()
        block_to_core(b).start()
    for k in x_far:
        b = other_x(k)
        copy(wobuf.at[x], wobuf.at[x], ws.at[b], wr.at[x], x=b).start()

    rows = 2 * group * ROWS
    pairs = nx // 2

    def attend(cc, p):
        token = (
            2 * p * per_x
            + lax.div(iota((rows, LANES), 0), group * ROWS) * per_x
            + cc * ROWS
            + lax.rem(iota((rows, LANES), 0), ROWS)
        )
        lane = iota((rows, LANES), 1)
        seen = jnp.logical_and(lane < tail, k_first + lane <= token)
        for g in range(kv):
            q = qbuf[cc, pl.ds(2 * p, 2), g * group : (g + 1) * group].reshape(rows, LANES)
            most = jnp.full((rows, LANES), negative, F32)
            for at in range(0, slots, KEYS):
                score = lax.dot_general(
                    q, ks[g, at : at + KEYS, :], (((1,), (1,)), ((), ())), preferred_element_type=F32
                )
                s_ref[g, :, at : at + KEYS] = score
                for lo in range(0, KEYS, LANES):
                    most = jnp.maximum(most, score[:, lo : lo + LANES])
            score = lax.dot_general(
                q, ks[g, slots:, :], (((1,), (1,)), ((), ())), preferred_element_type=F32
            )
            score = jnp.where(jnp.logical_and(seen, my_g == g), score, negative)
            most = jnp.max(jnp.maximum(most, score), axis=1, keepdims=True)
            acc = jnp.dot(
                jnp.exp(score - most).astype(BF16), vs[g, slots:, :], preferred_element_type=F32
            )
            for at in range(0, slots, KEYS):
                prob = jnp.exp(s_ref[g, :, at : at + KEYS] - most).astype(BF16)
                acc = acc + jnp.dot(prob, vs[g, at : at + KEYS, :], preferred_element_type=F32)
            sums = acc[:, LANES:]
            result = acc[:, 0:LANES] / sums
            lse = most + jnp.log(sums)
            for j in range(2):
                cut = slice(j * group * ROWS, (j + 1) * group * ROWS)
                ob[2 * p + j, g * group * ROWS : (g + 1) * group * ROWS, :] = result[cut]
                lb[2 * p + j, g : g + 1, :] = lse[cut].T[0:1]

    def core3(b):
        return (
            copy(obs.at[b], obr.at[b], c3s.at[b], c3r.at[b], c=sib),
            copy(lss.at[b], lsr.at[b], c3ls.at[b], c3lr.at[b], c=sib),
        )

    def combine(outs, logs):
        top = functools.reduce(jnp.maximum, logs)
        weights = [jnp.exp(v - top) for v in logs]
        whole = sum(weights)
        columns = as_columns(jnp.concatenate([w / whole for w in weights], 0))
        parts = []
        for g in range(kv):
            cut = slice(g * group * ROWS, (g + 1) * group * ROWS)
            parts.append(sum(columns[:, 8 * i + g : 8 * i + g + 1] * o[cut] for i, o in enumerate(outs)))
        return jnp.concatenate(parts, 0), top + jnp.log(whole)

    lb[...] = jnp.zeros_like(lb)
    for k in range(nx):
        b = other_x(k)
        copy(qbuf.at[sib, b], qbuf.at[sib, b], c2s.at[b], c2r.at[b], c=sib).wait_recv()

    def pair_of(j):
        return lax.rem(lax.div(x, 2) + 1 + j, pairs)

    def sibling_unit(j, _):
        p = pair_of(j)
        attend(sib, p)
        for i in range(2):
            b = 2 * p + i
            obs[b] = ob[b].astype(BF16)
            lss[b] = lb[b]
            for one in core3(b):
                one.start()
        return 0

    for j in range(pairs):
        sibling_unit(j, 0)

    def own_unit(j, _):
        p = pair_of(j)
        attend(c, p)
        for i in range(2):
            b = 2 * p + i
            for one in core3(b):
                one.wait_recv()
            out, lse = combine([ob[b], obr[b].astype(F32)], [lb[b], lsr[b]])
            ob[b] = out
            lb[b] = lse
            oxs[b] = out.astype(BF16)
            lxs[b] = lse

            @pl.when(b != x)
            def _():
                copy(oxs.at[b], oxr.at[x], x3s.at[b], x3r.at[x], x=b).start()
                copy(lxs.at[b], lxr.at[x], x3ls.at[b], x3lr.at[x], x=b).start()

        return 0

    for j in range(pairs):
        own_unit(j, 0)

    outs, logs = [ob[x]], [lb[x]]
    for k in x_near:
        b = other_x(k)
        copy(oxs.at[b], oxr.at[b], x3s.at[b], x3r.at[b], x=b).wait_recv()
        copy(lxs.at[b], lxr.at[b], x3ls.at[b], x3lr.at[b], x=b).wait_recv()
        outs.append(oxr[b].astype(F32))
        logs.append(lxr[b])
    out, lse = combine(outs, logs)
    ozs[...] = out.astype(BF16).reshape(nz, ROWS, LANES)
    lzs[...] = lse
    for k in z_far:
        b = other_z(k)
        copy(ozs.at[b], ozr.at[z], z3s.at[b], z3r.at[z], z=b).start()
        copy(lzs, lzr.at[z], z3ls.at[b], z3lr.at[z], z=b).start()

    outs, logs = [ozs[z].astype(F32)], [lzs[...]]
    for k in z_near:
        b = other_z(k)
        copy(ozs.at[b], ozr.at[b], z3s.at[b], z3r.at[b], z=b).wait_recv()
        copy(lzs, lzr.at[b], z3ls.at[b], z3lr.at[b], z=b).wait_recv()
        outs.append(ozr[b].astype(F32))
        logs.append(lzr[b])
    picked = []
    for v in logs:
        row = v[0:1]
        for g in range(1, kv):
            row = jnp.where(my_g == g, v[g : g + 1], row)
        picked.append(row)
    weights = jnp.concatenate(picked, 0)
    weights = jnp.exp(weights - jnp.max(weights, axis=0, keepdims=True))
    wt[...] = as_columns(weights / jnp.sum(weights, axis=0, keepdims=True))
    mine = wt[pl.ds(pl.multiple_of(my_quarter * ROWS, ROWS), ROWS), :]
    attended = sum(mine[:, i : i + 1] * o for i, o in enumerate(outs))
    att[c, z] = attended.astype(BF16)

    def piece_to_core(t):
        return copy(att.at[c, t], att.at[c, t], c4s.at[t], c4r.at[t], c=sib)

    for k in z_far:
        b = other_z(k)
        copy(att.at[c, z], att.at[c, z], z4s.at[b], z4r.at[z], z=b).start()
    piece_to_core(z).start()
    for k in x_near:
        b = other_x(k)
        copy(wobuf.at[b], wobuf.at[b], ws.at[b], wr.at[b], x=b).wait_recv()
    for k in z_near:
        b = other_z(k)
        copy(att.at[c, b], att.at[c, b], z4s.at[b], z4r.at[b], z=b).wait_recv()
        piece_to_core(b).start()
    for t in range(nz):
        copy(att.at[sib, t], att.at[sib, t], c4s.at[t], c4r.at[t], c=sib).wait_recv()

    per_half = heads // 2
    lhs = jnp.concatenate(
        [
            jnp.concatenate([att[cc, per_half * side + j] for j in range(per_half)], 1)
            for side in range(2)
            for cc in range(nc)
        ],
        0,
    )
    low = iota((ROWS, LANES), 1) < HALF
    for k in (*x_far, 0):
        b = other_x(k)
        got = jnp.dot(lhs, wobuf[b], preferred_element_type=F32)
        both = got[0:per_x] + pltpu.roll(got[per_x:], HALF, 1)
        packed = jnp.where(low, both[0:ROWS], pltpu.roll(both[ROWS:], HALF, 1))
        p5s[b] = packed.astype(BF16)
        last = copy(p5s.at[b], p5r.at[y], y5s.at[b], y5r.at[y], x=b, y=x)
        if k:
            last.start()
        else:

            @pl.when(x != y)
            def _():
                last.start()

            @pl.when(x == y)
            def _():
                p5r[y] = p5s[x]

    def arrival(b):
        return copy(p5s.at[y], p5r.at[b], y5s.at[y], y5r.at[b], x=y, y=b)

    for k in range(1, ny):
        arrival(lax.rem(y + k, ny)).wait_recv()

    @pl.when(x != y)
    def _():
        arrival(y).wait_recv()

    final = sum(p5r[b].astype(F32) for b in range(ny))
    out_ref[0:ROWS, :] = final[:, 0:HALF].astype(BF16)
    out_ref[ROWS:, :] = pltpu.roll(final, HALF, 1)[:, 0:HALF].astype(BF16)

    for b in range(nx):
        core1[b].wait_send()
        block_to_core(b).wait_send()
        for one in core3(b):
            one.wait_send()
    for k in range(1, nx):
        b = other_x(k)
        copy(xs.at[b], xr.at[x], x1s.at[b], x1r.at[x], x=b).wait_send()
        copy(wobuf.at[x], wobuf.at[x], ws.at[b], wr.at[x], x=b).wait_send()
        for t in range(nz):
            copy(qbuf.at[c, x, t], qbuf.at[c, x, t], x2s.at[b, t], x2r.at[x, t], x=b).wait_send()
        copy(oxs.at[b], oxr.at[x], x3s.at[b], x3r.at[x], x=b).wait_send()
        copy(lxs.at[b], lxr.at[x], x3ls.at[b], x3lr.at[x], x=b).wait_send()
        copy(p5s.at[b], p5r.at[y], y5s.at[b], y5r.at[y], x=b, y=x).wait_send()
    for k in range(1, nz):
        b = other_z(k)
        copy(zs.at[b], zr.at[z], z1s.at[b], z1r.at[z], z=b).wait_send()
        copy(qbuf.at[c, x, z], qbuf.at[c, x, z], z2s.at[b], z2r.at[z], z=b).wait_send()
        copy(ozs.at[b], ozr.at[z], z3s.at[b], z3r.at[z], z=b).wait_send()
        copy(lzs, lzr.at[z], z3ls.at[b], z3lr.at[z], z=b).wait_send()
        copy(att.at[c, z], att.at[c, z], z4s.at[b], z4r.at[z], z=b).wait_send()
    for t in range(nz):
        piece_to_core(t).wait_send()

    @pl.when(x != y)
    def _():
        copy(p5s.at[x], p5r.at[y], y5s.at[x], y5r.at[y], x=x, y=x).wait_send()


def local(
    sizes, hidden_in, norm_gain, w_query, w_key, w_value, w_out, cache_keys, cache_values, lengths, span_start
):
    nx, nz, nc, ny = sizes
    slots, kv, head_dim = cache_keys.shape
    span, own_cols = hidden_in.shape
    heads = w_query.shape[1] // head_dim
    assert head_dim == LANES and heads == nz and nc == 2 and span == nx * nc * ROWS and nx == ny
    assert w_out.shape[1] == HALF and slots % KEYS == 0 and kv == 2
    cols = w_query.shape[1] + 2 * w_key.shape[1] + LANES
    block = heads * ROWS
    piece = ROWS + 2 * (ROWS * kv // nz) + ROWS
    keys = slots + LANES
    rows = 2 * (heads // kv) * ROWS
    vmem = pl.BlockSpec(memory_space=pltpu.VMEM)
    smem = pl.BlockSpec(memory_space=pltpu.SMEM)
    hbm = pl.BlockSpec(memory_space=pltpu.HBM)
    V = pltpu.VMEM
    dma = pltpu.SemaphoreType.DMA
    scratch = [
        V((slots * kv, LANES), BF16), V((slots * kv, LANES), BF16), V((CHUNK * kv, LANES), F32),
        V((kv, keys, LANES), BF16), V((kv, keys, 2 * LANES), BF16),
        V((2, slots // CHUNK, LANES), F32), V((2, CHUNK, LANES), F32), V((kv, 8, LANES), F32),
        V((nx, ROWS, cols), BF16), V((nx, ROWS, cols), BF16), V((nx, ROWS, cols), F32),
        V((nx, ROWS, cols), BF16), V((nx, ROWS, cols), BF16),
        V((nz, piece, LANES), BF16), V((nz, piece, LANES), BF16), V((ROWS, LANES), F32),
        V((nc, nx, heads, ROWS, LANES), BF16), V((kv, rows, slots), F32),
        V((nx, block, LANES), F32), V((nx, 8, LANES), F32),
        V((nx, block, LANES), BF16), V((nx, block, LANES), BF16), V((nx, 8, LANES), F32), V((nx, 8, LANES), F32),
        V((nx, block, LANES), BF16), V((nx, block, LANES), BF16), V((nx, 8, LANES), F32), V((nx, 8, LANES), F32),
        V((nz, ROWS, LANES), BF16), V((nz, ROWS, LANES), BF16), V((8, LANES), F32), V((nz, 8, LANES), F32),
        V((LANES, LANES), F32),
        V((nc, heads, ROWS, LANES), BF16), V((nx, w_out.shape[0] // 2, LANES), BF16),
        V((nx, ROWS, LANES), BF16), V((ny, ROWS, LANES), BF16),
        dma((2,)),
        dma((nx,)), dma((nx,)), dma((nx,)), dma((nx,)), dma((nz,)), dma((nz,)),
        dma((nz,)), dma((nz,)), dma((nx, nz)), dma((nx, nz)), dma((nx,)), dma((nx,)), dma((nx,)), dma((nx,)),
        dma((nx,)), dma((nx,)), dma((nx,)), dma((nx,)), dma((nx,)), dma((nx,)), dma((nx,)), dma((nx,)),
        dma((nz,)), dma((nz,)), dma((nz,)), dma((nz,)),
        dma((nz,)), dma((nz,)), dma((nz,)), dma((nz,)), dma((nx,)), dma((ny,)),
    ]
    return pl.pallas_call(
        functools.partial(kernel, (nx, nz, nc, ny, nx * nz * nc * own_cols)),
        out_shape=jax.ShapeDtypeStruct((nc * ROWS, HALF), BF16),
        in_specs=[vmem] * 7 + [smem] * 2 + [hbm] * 2,
        out_specs=vmem,
        scratch_shapes=scratch,
        compiler_params=pltpu.CompilerParams(
            collective_id=0, has_side_effects=True, vmem_limit_bytes=60 * 1024 * 1024
        ),
    )(
        hidden_in, norm_gain, w_query, w_key, w_value, w_out, frequencies(), lengths, span_start,
        cache_keys.reshape(slots * kv, LANES), cache_values.reshape(slots * kv, LANES),
    )


def solution(mesh):
    physical = mesh.devices.shape
    ny = mesh.shape["head"]
    nc, nz = 2, 8
    nx = physical[0] // (nc * nz)
    finer = Mesh(mesh.devices.reshape(nx, nz, nc, ny), ("x", "z", "c", "y"))
    seq = ("x", "z", "c")
    return jax.shard_map(
        functools.partial(local, (nx, nz, nc, ny)),
        mesh=finer,
        in_specs=(
            P(None, seq), P(None, seq), P(seq, "y"), P(seq, "y"), P(seq, "y"), P("y", seq),
            P(seq, "y", None), P(seq, "y", None), P(), P(),
        ),
        out_specs=P("y", seq),
        check_vma=False,
    )
```

time: 254 us -> 73.9 us (0.29)
  blocking collectives: 74.8 us -> 0 us
  starting transfers between devices: 73.7 us -> 0 us
  Pallas kernels: 0 us -> 67.9 us
  waiting for transfers between devices: 67.4 us -> 0 us
  other arithmetic: 12.4 us -> 0.62 us
  local copies, waits for them, and re-layouts: 13.3 us -> 4.53 us
  matrix products: 7.33 us -> 0 us
    all_to_all x7 -> x0, blocking collectives: 74.8 us -> none  [the longest x3 37.6 us: sent_to_all(): return lax.all_to_all(copies, axis, split_axis=0, concat_axis=0, tiled=True)]
    all_to_all x5 -> x0, starting transfers between devices: 73.7 us -> none  [the longest x3 61.1 us: sent_to_all(): return lax.all_to_all(copies, axis, split_axis=0, concat_axis=0, tiled=True)]
    pallas_call x0 -> x1, Pallas kernels: none -> 67.9 us  [local(): pl.pallas_call(functools.partial(kernel, (nx, nz, nc, ny, nx * nz * nc *...]
    all_to_all x5 -> x0, waiting for transfers between devices: 67.4 us -> none  [the longest x3 40 us: sent_to_all(): return lax.all_to_all(copies, axis, split_axis=0, concat_axis=0, tiled=True)]
    dot_general x8 -> x0, matrix products: 7.33 us -> none  [the longest x2 3.82 us: attend(): jnp.einsum('grtk,kgd->grtd', probability.astype(jnp.bfloat16), value_bloc...]
    reduce_sum x11 -> x0, other arithmetic: 5.71 us -> none  [the longest x2 2.18 us: attend(): totals = totals * rescale + jnp.sum(probability, axis=-1)]
    unnamed x16 -> x3, local copies, waits for them, and re-layouts: 0.3 us -> 4.53 us
    mul x4 -> x0, other arithmetic: 3.24 us -> none  [the longest x3 2.58 us: rope_parts(): return (jnp.cos(angles) * mscale, jnp.sin(angles) * mscale)]
  transfers between devices with their start and end apart: 5 -> 0, of which waited for: 5 -> 0; matrix products, arithmetic and copies ran while one was open for 2% -> 0% of each run, Pallas kernels for 0% -> 0%
where the time goes in v1:
time: 73.9 us; the launch traced here: 73.7 us
  Pallas kernels  67.9 us (92%)
  local copies, waits for them, and re-layouts  4.53 us (6%)
    pallas_call x1, Pallas kernels, local(): pl.pallas_call(functools.partial(kernel, (nx, nz, nc, ny, nx * nz * nc *...  67.9 us
    unnamed x3, local copies, waits for them, and re-layouts  4.53 us

profile of v1, /device:TPU:1, one launch (start us, length us, event | category | flops | bytes accessed | tf_op | source)
XLA Modules:
  0.0 73.7 jit_solution(18217582406551557236)
XLA Ops:
  0.7 0.6 maximum_bitcast_fusion.freq_ref
  1.3 1.5 %copy.11.h_ref = bf16[256,64]{1,0:T(8,128)(2,1)} copy(bf16[256,64]{0,1:T(8,128)(2,1)} %param.10) | data formatting | bytes 65536 | tf_op args[0]
  2.7 1.7 %copy.12.wo_ref = bf16[1024,64]{1,0:T(8,128)(2,1)} copy(bf16[1024,64]{0,1:T(8,128)(2,1)} %param.15) | data formatting | bytes 262144 | tf_op args[5]
  4.5 67.9 %shard_map.100 = bf16[64,64]{1,0:T(8,128)(2,1)} custom-call(bf16[256,64]{1,0:T(8,128)(2,1)} %copy.11.h_ref, bf16[1,64]{1,0:T(2,128)(2,1)} %g_ref.1, bf16[64,1024]{1,0:T(8,128)(2,1)} %wq_ref.1, bf16[64,256]{1,0:T(8,128)(2,1)} %wk_ref.1, bf16[64,256]{1,0:T(8,128)(2,1)} %wv_ref.1, bf16[1024,64]{1,0:T(8,128)(2,1)} %copy.12.wo_ref, ...), custom_call_target="tpu_custom_call" | custom-call | tf_op jit(solution)/shard_map/pallas_call | solution.py:595
  72.3 1.3 %copy.15 = bf16[64,64]{1,0:T(8,128)(2,1)} copy(bf16[64,64]{1,0:T(8,128)(2,1)} %shard_map.100) | data formatting | bytes 16384
  (1 shorter events, 0.0 us)

commit v2 on v1

v2 whole, which is shorter than its diff:
```python
import functools
import math

import jax
import jax.numpy as jnp
import numpy as np
from jax import lax
from jax.experimental import pallas as pl
from jax.experimental.pallas import tpu as pltpu
from jax.sharding import Mesh
from jax.sharding import PartitionSpec as P

F32 = jnp.float32
BF16 = jnp.bfloat16
MESH = pl.DeviceIdType.MESH
LANES = 128
HALF = 64
ROWS = 32
CHUNK = 128
KEYS = 512

rope_base = 500000.0
stretch = 64.0
initial_context = 8192.0
ramp_low = 1.0
ramp_high = 32.0
epsilon = 1e-05
negative = -1e30
mscale = 0.1 * math.log(stretch) + 1.0


class Phases:
    def __init__(self):
        self.open = None

    def __call__(self, name):
        if self.open is not None:
            self.open.__exit__(None, None, None)
        self.open = None
        if name:
            self.open = jax.named_scope(name)
            self.open.__enter__()


def frequencies():
    base = rope_base ** (-2.0 * np.arange(HALF) / LANES)
    turns = initial_context * base / (2.0 * math.pi)
    share = np.clip((turns - ramp_low) / (ramp_high - ramp_low), 0.0, 1.0)
    freq = (1.0 - share) * base / stretch + share * base
    return np.concatenate([freq, freq])[None, :].astype(np.float32)


def cos_sin(angles):
    turns = jnp.floor(angles * (1.0 / (2.0 * math.pi)) + 0.5)
    first, second = 6.28125, 253.0 / 2.0**17
    third = 2.0 * math.pi - first - second
    rest = angles - turns * first - turns * second - turns * third
    return jnp.cos(rest), jnp.sin(rest)


def iota(shape, dim):
    return lax.broadcasted_iota(jnp.int32, shape, dim)


def signed(sine):
    return jnp.where(iota(sine.shape, 1) < HALF, -sine, sine)


def rotated(vectors, cosine, sine):
    return vectors * cosine + pltpu.roll(vectors, HALF, 1) * sine


def as_columns(rows):
    spare = LANES - rows.shape[0]
    if spare:
        rows = jnp.concatenate([rows, jnp.zeros((spare, LANES), F32)], 0)
    return rows.T


def kernel(
    dims,
    len_ref, start_ref, h_hbm, g_hbm, wq_hbm, wk_hbm, wv_hbm, wo_hbm, freq_hbm, k_hbm, v_hbm,
    out_ref,
    h_ref, g_ref, wq_ref, wk_ref, wv_ref, freq_ref, kraw, vraw, tmp, ks, vs, tab_a, tab_b,
    sb, rb, own, xs, xr, zs, zr, ssc, sscr, ssx, ssxr, ssz, sszr, qbuf, s_ref,
    ob, lb, obs, obr, lss, lsr, oxs, oxr, lxs, lxr, ozs, ozr, lzs, lzr, wt,
    att, wobuf, p5s, p5r,
    in_sem,
    c1s, c1r, x1s, x1r, z1s, z1r, css, csr, xss, xsr, zss, zsr,
    z2s, z2r, x2s, x2r, c2s, c2r, ws, wr, wcs, wcr,
    c3s, c3r, c3ls, c3lr, x3s, x3r, x3ls, x3lr, z3s, z3r, z3ls, z3lr,
    z4s, z4r, y5s, y5r,
):
    nx, nz, nc, ny, d_model = dims
    x, z, c, y = (lax.axis_index(n) for n in ("x", "z", "c", "y"))
    sib = 1 - c
    slots = kraw.shape[0] // 2
    group = wq_ref.shape[1] // wk_ref.shape[1]
    kv = wk_ref.shape[1] // LANES
    heads = kv * group
    quarters = nz // kv
    tail = ROWS // quarters
    qc = heads * LANES
    kc = kv * LANES
    per_x = nc * ROWS
    block = group * ROWS
    depth, span = h_ref.shape
    phase = Phases()

    def copy(src, dst, send, recv, **to):
        return pltpu.make_async_remote_copy(
            src_ref=src, dst_ref=dst, send_sem=send, recv_sem=recv, device_id=to, device_id_type=MESH
        )

    def other_x(k):
        return lax.rem(x + k, nx)

    def other_z(k):
        return lax.rem(z + k, nz)

    x_far = sorted(range(1, nx), key=lambda k: -min(k, nx - k))
    z_far = sorted(range(1, nz), key=lambda k: -min(k, nz - k))
    z_near = z_far[::-1]
    x_near = x_far[::-1]

    phase("entry")
    barrier = pltpu.get_barrier_semaphore()

    def greet(**to):
        pl.semaphore_signal(barrier, inc=1, device_id=to, device_id_type=MESH)

    for k in z_far:
        greet(z=other_z(k))
    for k in range(1, ny):
        for cc in range(nc):
            greet(x=y, y=lax.rem(y + k, ny), c=cc)

    @pl.when(x != y)
    def _():
        for cc in range(nc):
            greet(x=y, c=cc)

    for k in x_far:
        greet(x=other_x(k))
    greet(c=sib)

    fetches = []
    for i, (src, dst) in enumerate(
        (
            (h_hbm, h_ref), (g_hbm, g_ref), (wq_hbm, wq_ref), (wk_hbm, wk_ref), (wv_hbm, wv_ref),
            (freq_hbm, freq_ref), (k_hbm, kraw), (v_hbm, vraw), (wo_hbm, wobuf.at[x, c]),
        )
    ):
        fetches.append(pltpu.make_async_copy(src, dst, in_sem.at[i]))
        fetches[-1].start()
    get_h, get_g, get_wq, get_wk, get_wv, get_freq, get_k, get_v, get_wo = fetches

    my = (x * nz + z) * nc + c
    count = nx * nz * nc

    def add_lengths(r, carry):
        before, total = carry
        return before + jnp.where(r < my, len_ref[r], 0), total + len_ref[r]

    offset, first_pos = lax.fori_loop(0, count, add_lengths, (jnp.int32(0), jnp.int32(0)))
    first_pos = first_pos + start_ref[0]
    live = len_ref[my]

    get_h.wait()
    get_g.wait()
    hidden = h_ref[...].astype(F32)
    squares = jnp.sum(hidden * hidden, axis=0, keepdims=True)
    for r in range(span // LANES):
        ssc[r : r + 1, :] = squares[:, r * LANES : (r + 1) * LANES]
    gain = jnp.concatenate([g_ref[...].astype(F32), jnp.zeros((1, LANES - depth), F32)], 1)
    gain = jnp.broadcast_to(gain, (LANES, LANES)).T[0:depth, 0:1]
    scaled = jnp.concatenate([hidden * gain, jnp.zeros((LANES - depth, span), F32)], 0).T
    get_wq.wait()
    get_wk.wait()
    get_wv.wait()

    def project(cc, store):
        blocks = [
            jnp.where(cc == 0, scaled[b * per_x : b * per_x + ROWS], scaled[b * per_x + ROWS : (b + 1) * per_x])
            for b in range(nx)
        ]
        rows = jnp.concatenate(blocks, 0)[:, 0:depth].astype(BF16)
        for at, w in ((0, wq_ref), (qc, wk_ref), (qc + kc, wv_ref)):
            got = jnp.dot(rows, w[...], preferred_element_type=F32)
            for b in range(nx):
                store(b, at, got[b * ROWS : (b + 1) * ROWS])

    def to_sibling(b, at, value):
        sb[b, :, at : at + value.shape[1]] = value.astype(BF16)

    def to_own(b, at, value):
        own[b, :, at : at + value.shape[1]] = value

    project(sib, to_sibling)

    phase("barrier")
    peers = 1 + (nx - 1) + (nz - 1) + nc * (ny - 1)
    pl.semaphore_wait(barrier, jnp.where(x != y, peers + nc, peers))

    phase("core1_project")
    core1 = [copy(sb.at[b], rb.at[b], c1s.at[b], c1r.at[b], c=sib) for b in range(nx)]
    for b in range(nx):
        core1[b].start()
    sum_c = copy(ssc, sscr, css.at[0], csr.at[0], c=sib)
    sum_c.start()

    project(c, to_own)
    get_freq.wait()
    freq = freq_ref[...]

    phase("core1_wait")
    for b in range(nx):
        core1[b].wait_recv()
    for k in x_far:
        b = other_x(k)
        xs[b] = (own[b] + rb[b].astype(F32)).astype(BF16)
        copy(xs.at[b], xr.at[x], x1s.at[b], x1r.at[x], x=b).start()
    sum_c.wait_recv()
    ssx[...] = ssc[...] + sscr[...]
    for k in x_far:
        b = other_x(k)
        copy(ssx, ssxr.at[x], xss.at[b], xsr.at[x], x=b).start()

    phase("keys")
    a_count = slots // CHUNK
    a_pos = (offset + CHUNK * iota((a_count, LANES), 0)).astype(F32)
    a_cos, a_sin = cos_sin(a_pos * freq)
    tab_a[0] = a_cos * mscale
    tab_a[1] = a_sin * mscale
    b_cos, b_sin = cos_sin(iota((CHUNK, LANES), 0).astype(F32) * freq)
    tab_b[0] = b_cos
    tab_b[1] = b_sin
    first_token = x * per_x + c * ROWS
    my_g, my_quarter = lax.div(z, quarters), lax.rem(z, quarters)
    k_first = first_token + my_quarter * tail
    q_pos = (first_pos + first_token + iota((ROWS, LANES), 0)).astype(F32)
    q_cos, q_sin = cos_sin(q_pos * freq)
    k_pos = (first_pos + k_first + iota((tail, LANES), 0)).astype(F32)
    k_cos, k_sin = cos_sin(k_pos * freq)
    q_cos, q_sin = q_cos * mscale, signed(q_sin * mscale)
    k_cos, k_sin = k_cos * mscale, signed(k_sin * mscale)

    get_k.wait()

    def slot_angles(a, size):
        cos_a = tab_a[0, pl.ds(a, 1), :]
        sin_a = tab_a[1, pl.ds(a, 1), :]
        cos_b, sin_b = tab_b[0, 0:size, :], tab_b[1, 0:size, :]
        return cos_a * cos_b - sin_a * sin_b, signed(sin_a * cos_b + cos_a * sin_b)

    tmp[0, 0 : 8 * kv, :] = kraw[0 : 8 * kv, :].astype(F32)
    slot_cos, slot_sin = slot_angles(0, 8)
    head_keys = [
        rotated(tmp[0, pl.ds(g, 8, stride=kv), :], slot_cos, slot_sin)[0:1] for g in range(kv)
    ]

    def rotate_chunks(j, _):
        for u in range(2):
            a = 2 * j + u
            at = pl.multiple_of(a * CHUNK, CHUNK)
            tmp[u] = kraw[pl.ds(pl.multiple_of(2 * at, 2 * CHUNK), 2 * CHUNK), :].astype(F32)
            cosine, sine = slot_angles(a, CHUNK)
            alive = at + iota((CHUNK, LANES), 0) < live
            for g in range(kv):
                keys = rotated(tmp[u, pl.ds(g, CHUNK, stride=kv), :], cosine, sine)
                ks[g, pl.ds(at, CHUNK), :] = jnp.where(alive, keys, head_keys[g]).astype(BF16)
        return 0

    steps = a_count // 2
    early = steps * 3 // 4
    lax.fori_loop(0, early, rotate_chunks, 0)

    phase("x1_wait")
    gathered = own[x] + rb[x].astype(F32)
    for k in x_near:
        b = other_x(k)
        copy(xs.at[b], xr.at[b], x1s.at[b], x1r.at[b], x=b).wait_recv()
        gathered = gathered + xr[b].astype(F32)
    for t in range(nz):
        g, quarter = t // quarters, t % quarters
        zs[t, 0:ROWS, :] = gathered[:, t * LANES : (t + 1) * LANES].astype(BF16)
        pair = [
            gathered[quarter * tail : (quarter + 1) * tail, at + g * LANES : at + (g + 1) * LANES]
            for at in (qc, qc + kc)
        ]
        zs[t, ROWS : ROWS + 2 * tail, :] = jnp.concatenate(pair, 0).astype(BF16)
    for k in z_far:
        b = other_z(k)
        copy(zs.at[b], zr.at[z], z1s.at[b], z1r.at[z], z=b).start()
    squares = ssx[...]
    for k in x_near:
        b = other_x(k)
        copy(ssx, ssxr.at[b], xss.at[b], xsr.at[b], x=b).wait_recv()
        squares = squares + ssxr[b]
    ssz[...] = squares
    for k in z_far:
        b = other_z(k)
        copy(ssz, sszr.at[z], zss.at[b], zsr.at[z], z=b).start()

    phase("values")
    lax.fori_loop(early, steps, rotate_chunks, 0)
    get_v.wait()

    def value_chunks(j, _):
        for u in range(2):
            at = pl.multiple_of((2 * j + u) * CHUNK, CHUNK)
            tmp[u] = vraw[pl.ds(pl.multiple_of(2 * at, 2 * CHUNK), 2 * CHUNK), :].astype(F32)
            alive = at + iota((CHUNK, LANES), 0) < live
            ones = jnp.where(alive, 1.0, 0.0).astype(BF16)
            for g in range(kv):
                values = jnp.where(alive, tmp[u, pl.ds(g, CHUNK, stride=kv), :], 0.0)
                vs[g, pl.ds(at, CHUNK), 0:LANES] = values.astype(BF16)
                vs[g, pl.ds(at, CHUNK), LANES:] = ones
        return 0

    lax.fori_loop(0, steps, value_chunks, 0)
    get_wo.wait()

    phase("z1_wait")
    total = zs[z].astype(F32)
    for k in z_near:
        b = other_z(k)
        copy(zs.at[b], zr.at[b], z1s.at[b], z1r.at[b], z=b).wait_recv()
        total = total + zr[b].astype(F32)
    for k in z_near:
        b = other_z(k)
        copy(ssz, sszr.at[b], zss.at[b], zsr.at[b], z=b).wait_recv()
        squares = squares + sszr[b]
    wt[...] = as_columns(lax.rsqrt(squares * (1.0 / d_model) + epsilon))
    which = lax.div(first_token, LANES)
    lane = lax.rem(first_token, LANES)

    def inverse_of(at, size):
        cols = wt[pl.ds(pl.multiple_of(at, 8), size), :]
        picked = cols[:, 0:1]
        for r in range(1, span // LANES):
            picked = jnp.where(which == r, cols[:, r : r + 1], picked)
        return picked

    query = rotated(total[0:ROWS] * inverse_of(lane, ROWS), q_cos, q_sin) * LANES**-0.5
    qbuf[c, x, z] = query.astype(BF16)

    for k in z_far:
        b = other_z(k)
        copy(qbuf.at[c, x, z], qbuf.at[c, x, z], z2s.at[b], z2r.at[z], z=b).start()

    def piece_to_x(t):
        for k in x_far:
            b = other_x(k)
            copy(qbuf.at[c, x, t], qbuf.at[c, x, t], x2s.at[b, t], x2r.at[x, t], x=b).start()

    piece_to_x(z)

    phase("new_keys")
    inv_new = inverse_of(lane + my_quarter * tail, tail)
    new_k = (total[ROWS : ROWS + tail] * inv_new).astype(BF16).astype(F32)
    new_k = rotated(new_k, k_cos, k_sin)
    new_v = total[ROWS + tail : ROWS + 2 * tail] * inv_new
    empty = jnp.zeros((LANES - tail, LANES), F32)
    new_k = jnp.concatenate([new_k, empty], 0).astype(BF16)
    new_v = jnp.concatenate([new_v, empty], 0).astype(BF16)
    new_ones = jnp.where(iota((LANES, LANES), 0) < tail, 1.0, 0.0).astype(BF16)
    for g in range(kv):
        ks[g, slots:, :] = new_k
        vs[g, slots:, 0:LANES] = new_v
        vs[g, slots:, LANES:] = new_ones

    phase("z2_wait")
    for k in z_near:
        b = other_z(k)
        copy(qbuf.at[c, x, b], qbuf.at[c, x, b], z2s.at[b], z2r.at[b], z=b).wait_recv()
        piece_to_x(b)

    phase("x2_wait")

    def block_to_core(b):
        return copy(qbuf.at[c, b], qbuf.at[c, b], c2s.at[b], c2r.at[b], c=sib)

    block_to_core(x).start()
    for k in x_near:
        b = other_x(k)
        for t in range(nz):
            copy(qbuf.at[c, b, t], qbuf.at[c, b, t], x2s.at[b, t], x2r.at[b, t], x=b).wait_recv()
        block_to_core(b).start()
    for k in x_far:
        b = other_x(k)
        copy(wobuf.at[x, c], wobuf.at[x, c], ws.at[b], wr.at[x], x=b).start()

    def weights_to_core(b):
        return copy(wobuf.at[b, c], wobuf.at[b, c], wcs.at[b], wcr.at[b], c=sib)

    weights_to_core(x).start()

    rows = 2 * block
    apart = nx // 2
    pairs = [(i, i + apart) for i in range(apart)]

    def attend(cc, pair):
        blocks = [other_x(k) for k in pair]
        row = iota((rows, LANES), 0)
        token = jnp.where(row < block, blocks[0], blocks[1]) * per_x + cc * ROWS + lax.rem(row, ROWS)
        lane = iota((rows, LANES), 1)
        seen = jnp.logical_and(lane < tail, k_first + lane <= token)
        for g in range(kv):
            q = jnp.concatenate(
                [qbuf[cc, b, g * group : (g + 1) * group].reshape(block, LANES) for b in blocks], 0
            )
            most = jnp.full((rows, LANES), negative, F32)
            for at in range(0, slots, KEYS):
                score = lax.dot_general(
                    q, ks[g, at : at + KEYS, :], (((1,), (1,)), ((), ())), preferred_element_type=F32
                )
                s_ref[g, :, at : at + KEYS] = score
                for lo in range(0, KEYS, LANES):
                    most = jnp.maximum(most, score[:, lo : lo + LANES])
            score = lax.dot_general(
                q, ks[g, slots:, :], (((1,), (1,)), ((), ())), preferred_element_type=F32
            )
            score = jnp.where(jnp.logical_and(seen, my_g == g), score, negative)
            most = jnp.max(jnp.maximum(most, score), axis=1, keepdims=True)
            acc = jnp.dot(
                jnp.exp(score - most).astype(BF16), vs[g, slots:, :], preferred_element_type=F32
            )
            for at in range(0, slots, KEYS):
                prob = jnp.exp(s_ref[g, :, at : at + KEYS] - most).astype(BF16)
                acc = acc + jnp.dot(prob, vs[g, at : at + KEYS, :], preferred_element_type=F32)
            sums = acc[:, LANES:]
            result = acc[:, 0:LANES] / sums
            lse = most + jnp.log(sums)
            for j, b in enumerate(blocks):
                cut = slice(j * block, (j + 1) * block)
                yield b, g, result[cut], lse[cut].T[0:1]

    def core3(b):
        return (
            copy(obs.at[b], obr.at[b], c3s.at[b], c3r.at[b], c=sib),
            copy(lss.at[b], lsr.at[b], c3ls.at[b], c3lr.at[b], c=sib),
        )

    def combine(outs, logs):
        top = functools.reduce(jnp.maximum, logs)
        weights = [jnp.exp(v - top) for v in logs]
        whole = sum(weights)
        spare = jnp.zeros((8 - kv, LANES), F32)
        columns = as_columns(
            jnp.concatenate([jnp.concatenate([w / whole, spare], 0) for w in weights], 0)
        )
        parts = []
        for g in range(kv):
            cut = slice(g * block, (g + 1) * block)
            parts.append(sum(columns[:, 8 * i + g : 8 * i + g + 1] * o[cut] for i, o in enumerate(outs)))
        return jnp.concatenate(parts, 0), top + jnp.log(whole)

    def own_unit(pair):
        for b, g, result, lse in attend(c, pair):
            ob[b, g * block : (g + 1) * block, :] = result
            lb[b, g : g + 1, :] = lse

    def sibling_unit(pair):
        for b, g, result, lse in attend(sib, pair):
            obs[b, g * block : (g + 1) * block, :] = result.astype(BF16)
            lss[b, g : g + 1, :] = lse
        for k in pair:
            for one in core3(other_x(k)):
                one.start()

    def join_cores(pair):
        for k in pair:
            b = other_x(k)
            for one in core3(b):
                one.wait_recv()
            out, lse = combine([ob[b], obr[b].astype(F32)], [lb[b], lsr[b]])
            if k:
                oxs[b] = out.astype(BF16)
                lxs[b] = lse
                copy(oxs.at[b], oxr.at[x], x3s.at[b], x3r.at[x], x=b).start()
                copy(lxs.at[b], lxr.at[x], x3ls.at[b], x3lr.at[x], x=b).start()
            else:
                ob[b] = out
                lb[b] = lse

    phase("unit_0")
    own_unit(pairs[0])
    phase("c2_wait")
    for k in range(nx):
        b = other_x(k)
        copy(qbuf.at[sib, b], qbuf.at[sib, b], c2s.at[b], c2r.at[b], c=sib).wait_recv()
    for i, pair in enumerate(pairs):
        phase("unit_1")
        sibling_unit(pair)
        if i == 0:
            phase("weights")
            for k in x_near:
                b = other_x(k)
                copy(wobuf.at[b, c], wobuf.at[b, c], ws.at[b], wr.at[b], x=b).wait_recv()
                weights_to_core(b).start()
    phase("join")
    join_cores(pairs[0])
    for pair in pairs[1:]:
        phase("unit_2")
        own_unit(pair)
        phase("join_2")
        join_cores(pair)

    phase("x3_wait")
    outs, logs = [ob[x]], [lb[x]]
    for k in x_far:
        b = other_x(k)
        copy(oxs.at[b], oxr.at[b], x3s.at[b], x3r.at[b], x=b).wait_recv()
        copy(lxs.at[b], lxr.at[b], x3ls.at[b], x3lr.at[b], x=b).wait_recv()
        outs.append(oxr[b].astype(F32))
        logs.append(lxr[b])
    out, lse = combine(outs, logs)
    ozs[...] = out.astype(BF16).reshape(nz, ROWS, LANES)
    lzs[...] = lse
    for k in z_far:
        b = other_z(k)
        copy(ozs.at[b], ozr.at[z], z3s.at[b], z3r.at[z], z=b).start()
        copy(lzs, lzr.at[z], z3ls.at[b], z3lr.at[z], z=b).start()

    phase("z3_wait")
    outs, logs = [ozs[z].astype(F32)], [lzs[...]]
    for k in z_near:
        b = other_z(k)
        copy(ozs.at[b], ozr.at[b], z3s.at[b], z3r.at[b], z=b).wait_recv()
        copy(lzs, lzr.at[b], z3ls.at[b], z3lr.at[b], z=b).wait_recv()
        outs.append(ozr[b].astype(F32))
        logs.append(lzr[b])
    picked = []
    for v in logs:
        row = v[0:1]
        for g in range(1, kv):
            row = jnp.where(my_g == g, v[g : g + 1], row)
        picked.append(row)
    weights = jnp.concatenate(picked, 0)
    weights = jnp.exp(weights - jnp.max(weights, axis=0, keepdims=True))
    wt[...] = as_columns(weights / jnp.sum(weights, axis=0, keepdims=True))
    mine = wt[pl.ds(pl.multiple_of(my_quarter * ROWS, ROWS), ROWS), :]
    attended = sum(mine[:, i : i + 1] * o for i, o in enumerate(outs))
    att[z] = attended.astype(BF16)

    for k in z_far:
        b = other_z(k)
        copy(att.at[z], att.at[z], z4s.at[b], z4r.at[z], z=b).start()

    phase("z4_wait")
    for k in range(1, nx):
        b = other_x(k)
        copy(wobuf.at[b, sib], wobuf.at[b, sib], wcs.at[b], wcr.at[b], c=sib).wait_recv()
    copy(wobuf.at[x, sib], wobuf.at[x, sib], wcs.at[x], wcr.at[x], c=sib).wait_recv()
    for k in z_near:
        b = other_z(k)
        copy(att.at[b], att.at[b], z4s.at[b], z4r.at[b], z=b).wait_recv()

    phase("w_out")
    lhs = jnp.concatenate([att[t] for t in range(heads)], 1)
    rhs = wobuf[...].reshape(nx * nc * HALF, heads * LANES)
    got = lax.dot_general(lhs, rhs, (((1,), (1,)), ((), ())), preferred_element_type=F32)
    deep = ROWS // 2
    low = iota((deep, LANES), 1) < HALF
    for b in range(nx):
        both = got[:, b * LANES : (b + 1) * LANES]
        turned = pltpu.roll(both, HALF, 1)
        p5s[b, 0] = jnp.where(low, both[0:deep], turned[deep:]).astype(BF16)
        p5s[b, 1] = jnp.where(low, turned[0:deep], both[deep:]).astype(BF16)

    def last(b, cc):
        return copy(p5s.at[b, cc], p5r.at[c, y], y5s.at[b, cc], y5r.at[c, y], x=b, c=cc, y=x)

    for k in x_far:
        for cc in range(nc):
            last(other_x(k), cc).start()
    last(x, sib).start()

    @pl.when(x != y)
    def _():
        last(x, c).start()

    @pl.when(x == y)
    def _():
        p5r[c, y] = p5s[x, c]

    phase("y5_wait")

    def arrival(cc, b):
        return copy(p5s.at[y, cc], p5r.at[cc, b], y5s.at[y, cc], y5r.at[cc, b], x=y, c=cc, y=b)

    for k in range(1, ny):
        for cc in range(nc):
            arrival(cc, lax.rem(y + k, ny)).wait_recv()
    arrival(sib, y).wait_recv()

    @pl.when(x != y)
    def _():
        arrival(c, y).wait_recv()

    for cc in range(nc):
        final = sum(p5r[cc, b].astype(F32) for b in range(ny))
        at = cc * ROWS
        out_ref[at : at + deep, :] = final[:, 0:HALF].astype(BF16)
        out_ref[at + deep : at + ROWS, :] = pltpu.roll(final, HALF, 1)[:, 0:HALF].astype(BF16)

    phase("drain")
    sum_c.wait_send()
    for b in range(nx):
        core1[b].wait_send()
        block_to_core(b).wait_send()
        weights_to_core(b).wait_send()
        for one in core3(b):
            one.wait_send()
    for k in range(1, nx):
        b = other_x(k)
        copy(xs.at[b], xr.at[x], x1s.at[b], x1r.at[x], x=b).wait_send()
        copy(ssx, ssxr.at[x], xss.at[b], xsr.at[x], x=b).wait_send()
        copy(wobuf.at[x, c], wobuf.at[x, c], ws.at[b], wr.at[x], x=b).wait_send()
        for t in range(nz):
            copy(qbuf.at[c, x, t], qbuf.at[c, x, t], x2s.at[b, t], x2r.at[x, t], x=b).wait_send()
        copy(oxs.at[b], oxr.at[x], x3s.at[b], x3r.at[x], x=b).wait_send()
        copy(lxs.at[b], lxr.at[x], x3ls.at[b], x3lr.at[x], x=b).wait_send()
        for cc in range(nc):
            last(b, cc).wait_send()
    for k in range(1, nz):
        b = other_z(k)
        copy(zs.at[b], zr.at[z], z1s.at[b], z1r.at[z], z=b).wait_send()
        copy(ssz, sszr.at[z], zss.at[b], zsr.at[z], z=b).wait_send()
        copy(qbuf.at[c, x, z], qbuf.at[c, x, z], z2s.at[b], z2r.at[z], z=b).wait_send()
        copy(ozs.at[b], ozr.at[z], z3s.at[b], z3r.at[z], z=b).wait_send()
        copy(lzs, lzr.at[z], z3ls.at[b], z3lr.at[z], z=b).wait_send()
        copy(att.at[z], att.at[z], z4s.at[b], z4r.at[z], z=b).wait_send()
    last(x, sib).wait_send()

    @pl.when(x != y)
    def _():
        last(x, c).wait_send()

    phase(None)


def local(
    sizes, hidden_in, norm_gain, w_query, w_key, w_value, w_out, cache_keys, cache_values, lengths, span_start
):
    nx, nz, nc, ny = sizes
    slots, kv, head_dim = cache_keys.shape
    span, depth = hidden_in.shape
    heads = w_query.shape[1] // head_dim
    assert head_dim == LANES and heads == nz and nc == 2 and span == nx * nc * ROWS and nx == ny
    assert w_out.shape[1] == HALF and slots % KEYS == 0 and kv == 2
    cols = w_query.shape[1] + 2 * w_key.shape[1]
    block = heads * ROWS
    piece = ROWS + 2 * (ROWS * kv // nz)
    keys = slots + LANES
    rows = 2 * (heads // kv) * ROWS
    lines = span // LANES
    smem = pl.BlockSpec(memory_space=pltpu.SMEM)
    hbm = pl.BlockSpec(memory_space=pltpu.HBM)
    V = pltpu.VMEM
    dma = pltpu.SemaphoreType.DMA
    scratch = [
        V((depth, span), BF16), V((1, depth), BF16), V(w_query.shape, BF16), V(w_key.shape, BF16),
        V(w_value.shape, BF16), V((1, LANES), F32),
        V((slots * kv, LANES), BF16), V((slots * kv, LANES), BF16), V((2, CHUNK * kv, LANES), F32),
        V((kv, keys, LANES), BF16), V((kv, keys, 2 * LANES), BF16),
        V((2, slots // CHUNK, LANES), F32), V((2, CHUNK, LANES), F32),
        V((nx, ROWS, cols), BF16), V((nx, ROWS, cols), BF16), V((nx, ROWS, cols), F32),
        V((nx, ROWS, cols), BF16), V((nx, ROWS, cols), BF16),
        V((nz, piece, LANES), BF16), V((nz, piece, LANES), BF16),
        V((lines, LANES), F32), V((lines, LANES), F32), V((lines, LANES), F32), V((nx, lines, LANES), F32),
        V((lines, LANES), F32), V((nz, lines, LANES), F32),
        V((nc, nx, heads, ROWS, LANES), BF16), V((kv, rows, slots), F32),
        V((nx, block, LANES), F32), V((nx, kv, LANES), F32),
        V((nx, block, LANES), BF16), V((nx, block, LANES), BF16), V((nx, kv, LANES), F32), V((nx, kv, LANES), F32),
        V((nx, block, LANES), BF16), V((nx, block, LANES), BF16), V((nx, kv, LANES), F32), V((nx, kv, LANES), F32),
        V((nz, ROWS, LANES), BF16), V((nz, ROWS, LANES), BF16), V((kv, LANES), F32), V((nz, kv, LANES), F32),
        V((LANES, LANES), F32),
        V((heads, ROWS, LANES), BF16), V((nx, nc, HALF, w_out.shape[0]), BF16),
        V((nx, nc, ROWS // 2, LANES), BF16), V((nc, ny, ROWS // 2, LANES), BF16),
        dma((9,)),
        dma((nx,)), dma((nx,)), dma((nx,)), dma((nx,)), dma((nz,)), dma((nz,)),
        dma((1,)), dma((1,)), dma((nx,)), dma((nx,)), dma((nz,)), dma((nz,)),
        dma((nz,)), dma((nz,)), dma((nx, nz)), dma((nx, nz)), dma((nx,)), dma((nx,)),
        dma((nx,)), dma((nx,)), dma((nx,)), dma((nx,)),
        dma((nx,)), dma((nx,)), dma((nx,)), dma((nx,)), dma((nx,)), dma((nx,)), dma((nx,)), dma((nx,)),
        dma((nz,)), dma((nz,)), dma((nz,)), dma((nz,)),
        dma((nz,)), dma((nz,)), dma((nx, nc)), dma((nc, ny)),
    ]
    return pl.pallas_call(
        functools.partial(kernel, (nx, nz, nc, ny, nx * nz * nc * depth)),
        out_shape=jax.ShapeDtypeStruct((nc * ROWS, HALF), BF16),
        in_specs=[smem] * 2 + [hbm] * 9,
        out_specs=pl.BlockSpec(memory_space=pltpu.VMEM),
        scratch_shapes=scratch,
        compiler_params=pltpu.CompilerParams(
            collective_id=0, has_side_effects=True, vmem_limit_bytes=60 * 1024 * 1024
        ),
    )(
        lengths, span_start, hidden_in.T, norm_gain, w_query, w_key, w_value, w_out.T, frequencies(),
        cache_keys.reshape(slots * kv, LANES), cache_values.reshape(slots * kv, LANES),
    )


def solution(mesh):
    physical = mesh.devices.shape
    ny = mesh.shape["head"]
    nc, nz = 2, 8
    nx = physical[0] // (nc * nz)
    finer = Mesh(mesh.devices.reshape(nx, nz, nc, ny), ("x", "z", "c", "y"))
    seq = ("x", "z", "c")
    return jax.shard_map(
        functools.partial(local, (nx, nz, nc, ny)),
        mesh=finer,
        in_specs=(
            P(None, seq), P(None, seq), P(seq, "y"), P(seq, "y"), P(seq, "y"), P("y", seq),
            P(seq, "y", None), P(seq, "y", None), P(), P(),
        ),
        out_specs=P("y", seq),
        check_vma=False,
    )
```

time: 73.9 us -> 71.6 us (0.969)
  local copies, waits for them, and re-layouts: 4.53 us -> 1.32 us
  Pallas kernels: 67.9 us -> 69.4 us
    unnamed x3 -> x1, local copies, waits for them, and re-layouts: 4.53 us -> 1.32 us
    pallas_call x1, Pallas kernels: 67.9 us -> 69.4 us  [local(): pl.pallas_call(functools.partial(kernel, (nx, nz, nc, ny, nx * nz * nc *...]
where the time goes in v2:
time: 71.6 us; the launch traced here: 71.4 us
  Pallas kernels  69.4 us (97%)
  local copies, waits for them, and re-layouts  1.32 us (2%)
    pallas_call x1, Pallas kernels, local(): pl.pallas_call(functools.partial(kernel, (nx, nz, nc, ny, nx * nz * nc *...  69.4 us

profile of v2, /device:TPU:1, one launch (start us, length us, event | category | flops | bytes accessed | tf_op | source)
XLA Modules:
  0.0 71.4 jit_solution(12254689272888816603)
XLA Ops:
  0.7 69.4 %shard_map.109 = bf16[64,64]{1,0:T(8,128)(2,1)} custom-call(s32[64]{0:T(128)} %len_ref.1, s32[1]{0:T(128)S(6)} %copy.13.start_ref, bf16[64,256]{1,0:T(8,128)(2,1)} %bitcast.7, bf16[1,64]{1,0:T(2,128)(2,1)} %g_hbm.1, bf16[64,1024]{1,0:T(8,128)(2,1)} %wq_hbm.1, bf16[64,256]{1,0:T(8,128)(2,1)} %wk_hbm.1, bf16[64,256]{1,0:T(8,128)(2,1)} %wv_hbm.1, ...), custom_call_target="tpu_custom_call" | custom-call | tf_op jit(solution)/shard_map/pallas_call | solution.py:691
  70.1 1.3 %copy.14 = bf16[64,64]{1,0:T(8,128)(2,1)} copy(bf16[64,64]{1,0:T(8,128)(2,1)} %shard_map.109) | data formatting | bytes 16384

commit v3 on v2

--- a/solution.py
+++ b/solution.py
@@ -79,16 +79,18 @@
 
 def kernel(
     dims,
-    len_ref, start_ref, h_hbm, g_hbm, wq_hbm, wk_hbm, wv_hbm, wo_hbm, freq_hbm, k_hbm, v_hbm,
+    len_hbm, start_hbm, h_hbm, g_hbm, wq_hbm, wk_hbm, wv_hbm, wo_hbm, freq_hbm, k_hbm, v_hbm,
     out_ref,
+    len_ref, start_ref,
     h_ref, g_ref, wq_ref, wk_ref, wv_ref, freq_ref, kraw, vraw, tmp, ks, vs, tab_a, tab_b,
-    sb, rb, own, xs, xr, zs, zr, ssc, sscr, ssx, ssxr, ssz, sszr, qbuf, s_ref,
-    ob, lb, obs, obr, lss, lsr, oxs, oxr, lxs, lxr, ozs, ozr, lzs, lzr, wt,
+    sb, rb, own, xs, xr, zs, zr, sb2, rb2, own2, xs2, xr2, zs2, zr2,
+    ssc, sscr, ssx, ssxr, ssz, sszr, qbuf, s_ref,
+    ob, lb, obs, obr, lss, lsr, oxs, oxr, lxs, lxr, wt,
     att, wobuf, p5s, p5r,
     in_sem,
-    c1s, c1r, x1s, x1r, z1s, z1r, css, csr, xss, xsr, zss, zsr,
+    c1s, c1r, x1s, x1r, z1s, z1r, d1s, d1r, w1s, w1r, v1s, v1r, css, csr, xss, xsr, zss, zsr,
     z2s, z2r, x2s, x2r, c2s, c2r, ws, wr, wcs, wcr,
-    c3s, c3r, c3ls, c3lr, x3s, x3r, x3ls, x3lr, z3s, z3r, z3ls, z3lr,
+    c3s, c3r, c3ls, c3lr, x3s, x3r, x3ls, x3lr,
     z4s, z4r, y5s, y5r,
 ):
     nx, nz, nc, ny, d_model = dims
@@ -148,23 +150,13 @@
     for i, (src, dst) in enumerate(
         (
             (h_hbm, h_ref), (g_hbm, g_ref), (wq_hbm, wq_ref), (wk_hbm, wk_ref), (wv_hbm, wv_ref),
-            (freq_hbm, freq_ref), (k_hbm, kraw), (v_hbm, vraw), (wo_hbm, wobuf.at[x, c]),
+            (freq_hbm, freq_ref), (len_hbm, len_ref), (start_hbm, start_ref),
+            (k_hbm, kraw), (v_hbm, vraw), (wo_hbm, wobuf.at[x, c]),
         )
     ):
         fetches.append(pltpu.make_async_copy(src, dst, in_sem.at[i]))
         fetches[-1].start()
-    get_h, get_g, get_wq, get_wk, get_wv, get_freq, get_k, get_v, get_wo = fetches
-
-    my = (x * nz + z) * nc + c
-    count = nx * nz * nc
-
-    def add_lengths(r, carry):
-        before, total = carry
-        return before + jnp.where(r < my, len_ref[r], 0), total + len_ref[r]
-
-    offset, first_pos = lax.fori_loop(0, count, add_lengths, (jnp.int32(0), jnp.int32(0)))
-    first_pos = first_pos + start_ref[0]
-    live = len_ref[my]
+    get_h, get_g, get_wq, get_wk, get_wv, get_freq, get_len, get_start, get_k, get_v, get_wo = fetches
 
     get_h.wait()
     get_g.wait()
@@ -179,24 +171,23 @@
     get_wk.wait()
     get_wv.wait()
 
-    def project(cc, store):
+    def rows_of(cc):
         blocks = [
             jnp.where(cc == 0, scaled[b * per_x : b * per_x + ROWS], scaled[b * per_x + ROWS : (b + 1) * per_x])
             for b in range(nx)
         ]
-        rows = jnp.concatenate(blocks, 0)[:, 0:depth].astype(BF16)
-        for at, w in ((0, wq_ref), (qc, wk_ref), (qc + kc, wv_ref)):
+        return jnp.concatenate(blocks, 0)[:, 0:depth].astype(BF16)
+
+    def project(rows, weights, to):
+        at = 0
+        for w in weights:
             got = jnp.dot(rows, w[...], preferred_element_type=F32)
             for b in range(nx):
-                store(b, at, got[b * ROWS : (b + 1) * ROWS])
-
-    def to_sibling(b, at, value):
-        sb[b, :, at : at + value.shape[1]] = value.astype(BF16)
-
-    def to_own(b, at, value):
-        own[b, :, at : at + value.shape[1]] = value
-
-    project(sib, to_sibling)
+                to[b, :, at : at + got.shape[1]] = got[b * ROWS : (b + 1) * ROWS].astype(to.dtype)
+            at += got.shape[1]
+
+    project(rows_of(sib), (wq_ref,), sb)
+    project(rows_of(sib), (wk_ref, wv_ref), sb2)
 
     phase("barrier")
     peers = 1 + (nx - 1) + (nz - 1) + nc * (ny - 1)
@@ -204,12 +195,13 @@
 
     phase("core1_project")
     core1 = [copy(sb.at[b], rb.at[b], c1s.at[b], c1r.at[b], c=sib) for b in range(nx)]
-    for b in range(nx):
-        core1[b].start()
+    core2 = [copy(sb2.at[b], rb2.at[b], d1s.at[b], d1r.at[b], c=sib) for b in range(nx)]
     sum_c = copy(ssc, sscr, css.at[0], csr.at[0], c=sib)
-    sum_c.start()
-
-    project(c, to_own)
+    for one in (*core1, sum_c, *core2):
+        one.start()
+
+    project(rows_of(c), (wq_ref,), own)
+    project(rows_of(c), (wk_ref, wv_ref), own2)
     get_freq.wait()
     freq = freq_ref[...]
 
@@ -227,6 +219,19 @@
         copy(ssx, ssxr.at[x], xss.at[b], xsr.at[x], x=b).start()
 
     phase("keys")
+    get_len.wait()
+    get_start.wait()
+    my = (x * nz + z) * nc + c
+    count = nx * nz * nc
+
+    def add_lengths(r, carry):
+        before, total = carry
+        return before + jnp.where(r < my, len_ref[r], 0), total + len_ref[r]
+
+    offset, first_pos = lax.fori_loop(0, count, add_lengths, (jnp.int32(0), jnp.int32(0)))
+    first_pos = first_pos + start_ref[0]
+    live = len_ref[my]
+
     a_count = slots // CHUNK
     a_pos = (offset + CHUNK * iota((a_count, LANES), 0)).astype(F32)
     a_cos, a_sin = cos_sin(a_pos * freq)
@@ -282,13 +287,7 @@
         copy(xs.at[b], xr.at[b], x1s.at[b], x1r.at[b], x=b).wait_recv()
         gathered = gathered + xr[b].astype(F32)
     for t in range(nz):
-        g, quarter = t // quarters, t % quarters
-        zs[t, 0:ROWS, :] = gathered[:, t * LANES : (t + 1) * LANES].astype(BF16)
-        pair = [
-            gathered[quarter * tail : (quarter + 1) * tail, at + g * LANES : at + (g + 1) * LANES]
-            for at in (qc, qc + kc)
-        ]
-        zs[t, ROWS : ROWS + 2 * tail, :] = jnp.concatenate(pair, 0).astype(BF16)
+        zs[t] = gathered[:, t * LANES : (t + 1) * LANES].astype(BF16)
     for k in z_far:
         b = other_z(k)
         copy(zs.at[b], zr.at[z], z1s.at[b], z1r.at[z], z=b).start()
@@ -301,6 +300,13 @@
     for k in z_far:
         b = other_z(k)
         copy(ssz, sszr.at[z], zss.at[b], zsr.at[z], z=b).start()
+
+    for b in range(nx):
+        core2[b].wait_recv()
+    for k in x_far:
+        b = other_x(k)
+        xs2[b] = (own2[b] + rb2[b].astype(F32)).astype(BF16)
+        copy(xs2.at[b], xr2.at[x], w1s.at[b], w1r.at[x], x=b).start()
 
     phase("values")
     lax.fori_loop(early, steps, rotate_chunks, 0)
@@ -342,7 +348,7 @@
             picked = jnp.where(which == r, cols[:, r : r + 1], picked)
         return picked
 
-    query = rotated(total[0:ROWS] * inverse_of(lane, ROWS), q_cos, q_sin) * LANES**-0.5
+    query = rotated(total * inverse_of(lane, ROWS), q_cos, q_sin) * LANES**-0.5
     qbuf[c, x, z] = query.astype(BF16)
 
     for k in z_far:
@@ -357,10 +363,58 @@
     piece_to_x(z)
 
     phase("new_keys")
+    gathered = own2[x] + rb2[x].astype(F32)
+    for k in x_near:
+        b = other_x(k)
+        copy(xs2.at[b], xr2.at[b], w1s.at[b], w1r.at[b], x=b).wait_recv()
+        gathered = gathered + xr2[b].astype(F32)
+    for t in range(nz):
+        g, quarter = t // quarters, t % quarters
+        pair = [
+            gathered[quarter * tail : (quarter + 1) * tail, at + g * LANES : at + (g + 1) * LANES]
+            for at in (0, kc)
+        ]
+        zs2[t] = jnp.concatenate(pair, 0).astype(BF16)
+    for k in z_far:
+        b = other_z(k)
+        copy(zs2.at[b], zr2.at[z], v1s.at[b], v1r.at[z], z=b).start()
+
+    phase("z2_wait")
+    for k in z_near:
+        b = other_z(k)
+        copy(qbuf.at[c, x, b], qbuf.at[c, x, b], z2s.at[b], z2r.at[b], z=b).wait_recv()
+        piece_to_x(b)
+
+    phase("x2_wait")
+
+    def block_to_core(b):
+        return copy(qbuf.at[c, b], qbuf.at[c, b], c2s.at[b], c2r.at[b], c=sib)
+
+    block_to_core(x).start()
+    for k in x_near:
+        b = other_x(k)
+        for t in range(nz):
+            copy(qbuf.at[c, b, t], qbuf.at[c, b, t], x2s.at[b, t], x2r.at[b, t], x=b).wait_recv()
+        block_to_core(b).start()
+    for k in x_far:
+        b = other_x(k)
+        copy(wobuf.at[x, c], wobuf.at[x, c], ws.at[b], wr.at[x], x=b).start()
+
+    def weights_to_core(b):
+        return copy(wobuf.at[b, c], wobuf.at[b, c], wcs.at[b], wcr.at[b], c=sib)
+
+    weights_to_core(x).start()
+
+    phase("new_keys_wait")
+    total = zs2[z].astype(F32)
+    for k in z_near:
+        b = other_z(k)
+        copy(zs2.at[b], zr2.at[b], v1s.at[b], v1r.at[b], z=b).wait_recv()
+        total = total + zr2[b].astype(F32)
     inv_new = inverse_of(lane + my_quarter * tail, tail)
-    new_k = (total[ROWS : ROWS + tail] * inv_new).astype(BF16).astype(F32)
+    new_k = (total[0:tail] * inv_new).astype(BF16).astype(F32)
     new_k = rotated(new_k, k_cos, k_sin)
-    new_v = total[ROWS + tail : ROWS + 2 * tail] * inv_new
+    new_v = total[tail:] * inv_new
     empty = jnp.zeros((LANES - tail, LANES), F32)
     new_k = jnp.concatenate([new_k, empty], 0).astype(BF16)
     new_v = jnp.concatenate([new_v, empty], 0).astype(BF16)
@@ -369,32 +423,6 @@
         ks[g, slots:, :] = new_k
         vs[g, slots:, 0:LANES] = new_v
         vs[g, slots:, LANES:] = new_ones
-
-    phase("z2_wait")
-    for k in z_near:
-        b = other_z(k)
-        copy(qbuf.at[c, x, b], qbuf.at[c, x, b], z2s.at[b], z2r.at[b], z=b).wait_recv()
-        piece_to_x(b)
-
-    phase("x2_wait")
-
-    def block_to_core(b):
-        return copy(qbuf.at[c, b], qbuf.at[c, b], c2s.at[b], c2r.at[b], c=sib)
-
-    block_to_core(x).start()
-    for k in x_near:
-        b = other_x(k)
-        for t in range(nz):
-            copy(qbuf.at[c, b, t], qbuf.at[c, b, t], x2s.at[b, t], x2r.at[b, t], x=b).wait_recv()
-        block_to_core(b).start()
-    for k in x_far:
-        b = other_x(k)
-        copy(wobuf.at[x, c], wobuf.at[x, c], ws.at[b], wr.at[x], x=b).start()
-
-    def weights_to_core(b):
-        return copy(wobuf.at[b, c], wobuf.at[b, c], wcs.at[b], wcr.at[b], c=sib)
-
-    weights_to_core(x).start()
 
     rows = 2 * block
     apart = nx // 2
@@ -469,20 +497,37 @@
             for one in core3(other_x(k)):
                 one.start()
 
+    away = sorted(
+        ((i, j) for i in range(nx) for j in range(nz)),
+        key=lambda k: -min(k[0], nx - k[0]) - min(k[1], nz - k[1]),
+    )
+
+    def piece3(i, j):
+        b, t = other_x(i), other_z(j)
+        return (
+            copy(oxs.at[b, t], oxr.at[x, z], x3s.at[b, t], x3r.at[x, z], x=b, z=t),
+            copy(lxs.at[b], lxr.at[x, z], x3ls.at[b, t], x3lr.at[x, z], x=b, z=t),
+        )
+
+    def arrival3(i, j):
+        b, t = other_x(i), other_z(j)
+        return (
+            copy(oxs.at[b, t], oxr.at[b, t], x3s.at[b, t], x3r.at[b, t], x=b, z=t),
+            copy(lxs.at[b], lxr.at[b, t], x3ls.at[b, t], x3lr.at[b, t], x=b, z=t),
+        )
+
     def join_cores(pair):
         for k in pair:
             b = other_x(k)
             for one in core3(b):
                 one.wait_recv()
             out, lse = combine([ob[b], obr[b].astype(F32)], [lb[b], lsr[b]])
-            if k:
-                oxs[b] = out.astype(BF16)
-                lxs[b] = lse
-                copy(oxs.at[b], oxr.at[x], x3s.at[b], x3r.at[x], x=b).start()
-                copy(lxs.at[b], lxr.at[x], x3ls.at[b], x3lr.at[x], x=b).start()
-            else:
-                ob[b] = out
-                lb[b] = lse
+            oxs[b] = out.astype(BF16).reshape(nz, ROWS, LANES)
+            lxs[b] = lse
+        for i, j in away:
+            if i in pair and (i or j):
+                for one in piece3(i, j):
+                    one.start()
 
     phase("unit_0")
     own_unit(pairs[0])
@@ -508,29 +553,14 @@
         join_cores(pair)
 
     phase("x3_wait")
-    outs, logs = [ob[x]], [lb[x]]
-    for k in x_far:
-        b = other_x(k)
-        copy(oxs.at[b], oxr.at[b], x3s.at[b], x3r.at[b], x=b).wait_recv()
-        copy(lxs.at[b], lxr.at[b], x3ls.at[b], x3lr.at[b], x=b).wait_recv()
-        outs.append(oxr[b].astype(F32))
-        logs.append(lxr[b])
-    out, lse = combine(outs, logs)
-    ozs[...] = out.astype(BF16).reshape(nz, ROWS, LANES)
-    lzs[...] = lse
-    for k in z_far:
-        b = other_z(k)
-        copy(ozs.at[b], ozr.at[z], z3s.at[b], z3r.at[z], z=b).start()
-        copy(lzs, lzr.at[z], z3ls.at[b], z3lr.at[z], z=b).start()
-
-    phase("z3_wait")
-    outs, logs = [ozs[z].astype(F32)], [lzs[...]]
-    for k in z_near:
-        b = other_z(k)
-        copy(ozs.at[b], ozr.at[b], z3s.at[b], z3r.at[b], z=b).wait_recv()
-        copy(lzs, lzr.at[b], z3ls.at[b], z3lr.at[b], z=b).wait_recv()
-        outs.append(ozr[b].astype(F32))
-        logs.append(lzr[b])
+    outs, logs = [oxs[x, z]], [lxs[x]]
+    for i, j in away[::-1]:
+        if i or j:
+            for one in arrival3(i, j):
+                one.wait_recv()
+            outs.append(oxr[other_x(i), other_z(j)])
+            logs.append(lxr[other_x(i), other_z(j)])
+    phase("combine")
     picked = []
     for v in logs:
         row = v[0:1]
@@ -541,7 +571,7 @@
     weights = jnp.exp(weights - jnp.max(weights, axis=0, keepdims=True))
     wt[...] = as_columns(weights / jnp.sum(weights, axis=0, keepdims=True))
     mine = wt[pl.ds(pl.multiple_of(my_quarter * ROWS, ROWS), ROWS), :]
-    attended = sum(mine[:, i : i + 1] * o for i, o in enumerate(outs))
+    attended = sum(mine[:, i : i + 1] * o.astype(F32) for i, o in enumerate(outs))
     att[z] = attended.astype(BF16)
 
     for k in z_far:
@@ -609,6 +639,7 @@
     sum_c.wait_send()
     for b in range(nx):
         core1[b].wait_send()
+        core2[b].wait_send()
         block_to_core(b).wait_send()
         weights_to_core(b).wait_send()
         for one in core3(b):
@@ -620,8 +651,7 @@
         copy(wobuf.at[x, c], wobuf.at[x, c], ws.at[b], wr.at[x], x=b).wait_send()
         for t in range(nz):
             copy(qbuf.at[c, x, t], qbuf.at[c, x, t], x2s.at[b, t], x2r.at[x, t], x=b).wait_send()
-        copy(oxs.at[b], oxr.at[x], x3s.at[b], x3r.at[x], x=b).wait_send()
-        copy(lxs.at[b], lxr.at[x], x3ls.at[b], x3lr.at[x], x=b).wait_send()
+        copy(xs2.at[b], xr2.at[x], w1s.at[b], w1r.at[x], x=b).wait_send()
         for cc in range(nc):
             last(b, cc).wait_send()
     for k in range(1, nz):
@@ -629,10 +659,13 @@
         copy(zs.at[b], zr.at[z], z1s.at[b], z1r.at[z], z=b).wait_send()
         copy(ssz, sszr.at[z], zss.at[b], zsr.at[z], z=b).wait_send()
         copy(qbuf.at[c, x, z], qbuf.at[c, x, z], z2s.at[b], z2r.at[z], z=b).wait_send()
-        copy(ozs.at[b], ozr.at[z], z3s.at[b], z3r.at[z], z=b).wait_send()
-        copy(lzs, lzr.at[z], z3ls.at[b], z3lr.at[z], z=b).wait_send()
+        copy(zs2.at[b], zr2.at[z], v1s.at[b], v1r.at[z], z=b).wait_send()
         copy(att.at[z], att.at[z], z4s.at[b], z4r.at[z], z=b).wait_send()
     last(x, sib).wait_send()
+    for i, j in away:
+        if i or j:
+            for one in piece3(i, j):
+                one.wait_send()
 
     @pl.when(x != y)
     def _():
@@ -650,17 +683,17 @@
     heads = w_query.shape[1] // head_dim
     assert head_dim == LANES and heads == nz and nc == 2 and span == nx * nc * ROWS and nx == ny
     assert w_out.shape[1] == HALF and slots % KEYS == 0 and kv == 2
-    cols = w_query.shape[1] + 2 * w_key.shape[1]
+    cols, cols2 = w_query.shape[1], 2 * w_key.shape[1]
     block = heads * ROWS
-    piece = ROWS + 2 * (ROWS * kv // nz)
+    piece = 2 * (ROWS * kv // nz)
     keys = slots + LANES
     rows = 2 * (heads // kv) * ROWS
     lines = span // LANES
-    smem = pl.BlockSpec(memory_space=pltpu.SMEM)
     hbm = pl.BlockSpec(memory_space=pltpu.HBM)
     V = pltpu.VMEM
     dma = pltpu.SemaphoreType.DMA
     scratch = [
+        pltpu.SMEM(lengths.shape, jnp.int32), pltpu.SMEM(span_start.shape, jnp.int32),
         V((depth, span), BF16), V((1, depth), BF16), V(w_query.shape, BF16), V(w_key.shape, BF16),
         V(w_value.shape, BF16), V((1, LANES), F32),
         V((slots * kv, LANES), BF16), V((slots * kv, LANES), BF16), V((2, CHUNK * kv, LANES), F32),
@@ -668,30 +701,34 @@
         V((2, slots // CHUNK, LANES), F32), V((2, CHUNK, LANES), F32),
         V((nx, ROWS, cols), BF16), V((nx, ROWS, cols), BF16), V((nx, ROWS, cols), F32),
         V((nx, ROWS, cols), BF16), V((nx, ROWS, cols), BF16),
+        V((nz, ROWS, LANES), BF16), V((nz, ROWS, LANES), BF16),
+        V((nx, ROWS, cols2), BF16), V((nx, ROWS, cols2), BF16), V((nx, ROWS, cols2), F32),
+        V((nx, ROWS, cols2), BF16), V((nx, ROWS, cols2), BF16),
         V((nz, piece, LANES), BF16), V((nz, piece, LANES), BF16),
         V((lines, LANES), F32), V((lines, LANES), F32), V((lines, LANES), F32), V((nx, lines, LANES), F32),
         V((lines, LANES), F32), V((nz, lines, LANES), F32),
         V((nc, nx, heads, ROWS, LANES), BF16), V((kv, rows, slots), F32),
         V((nx, block, LANES), F32), V((nx, kv, LANES), F32),
         V((nx, block, LANES), BF16), V((nx, block, LANES), BF16), V((nx, kv, LANES), F32), V((nx, kv, LANES), F32),
-        V((nx, block, LANES), BF16), V((nx, block, LANES), BF16), V((nx, kv, LANES), F32), V((nx, kv, LANES), F32),
-        V((nz, ROWS, LANES), BF16), V((nz, ROWS, LANES), BF16), V((kv, LANES), F32), V((nz, kv, LANES), F32),
+        V((nx, nz, ROWS, LANES), BF16), V((nx, nz, ROWS, LANES), BF16),
+        V((nx, kv, LANES), F32), V((nx, nz, kv, LANES), F32),
         V((LANES, LANES), F32),
         V((heads, ROWS, LANES), BF16), V((nx, nc, HALF, w_out.shape[0]), BF16),
         V((nx, nc, ROWS // 2, LANES), BF16), V((nc, ny, ROWS // 2, LANES), BF16),
-        dma((9,)),
+        dma((11,)),
+        dma((nx,)), dma((nx,)), dma((nx,)), dma((nx,)), dma((nz,)), dma((nz,)),
         dma((nx,)), dma((nx,)), dma((nx,)), dma((nx,)), dma((nz,)), dma((nz,)),
         dma((1,)), dma((1,)), dma((nx,)), dma((nx,)), dma((nz,)), dma((nz,)),
         dma((nz,)), dma((nz,)), dma((nx, nz)), dma((nx, nz)), dma((nx,)), dma((nx,)),
         dma((nx,)), dma((nx,)), dma((nx,)), dma((nx,)),
-        dma((nx,)), dma((nx,)), dma((nx,)), dma((nx,)), dma((nx,)), dma((nx,)), dma((nx,)), dma((nx,)),
-        dma((nz,)), dma((nz,)), dma((nz,)), dma((nz,)),
+        dma((nx,)), dma((nx,)), dma((nx,)), dma((nx,)),
+        dma((nx, nz)), dma((nx, nz)), dma((nx, nz)), dma((nx, nz)),
         dma((nz,)), dma((nz,)), dma((nx, nc)), dma((nc, ny)),
     ]
     return pl.pallas_call(
         functools.partial(kernel, (nx, nz, nc, ny, nx * nz * nc * depth)),
-        out_shape=jax.ShapeDtypeStruct((nc * ROWS, HALF), BF16),
-        in_specs=[smem] * 2 + [hbm] * 9,
+        out_shape=pltpu.VMEM((nc * ROWS, HALF), BF16),
+        in_specs=[hbm] * 11,
         out_specs=pl.BlockSpec(memory_space=pltpu.VMEM),
         scratch_shapes=scratch,
         compiler_params=pltpu.CompilerParams(

time: 71.6 us -> 64.6 us (0.902)
  Pallas kernels: 69.4 us -> 63.2 us
    pallas_call x1, Pallas kernels: 69.4 us -> 63.2 us  [local(): pl.pallas_call(functools.partial(kernel, (nx, nz, nc, ny, nx * nz * nc *...]
    unnamed x1, local copies, waits for them, and re-layouts: 1.32 us -> 0.61 us
where the time goes in v3:
time: 64.6 us; the launch traced here: 64.5 us
  Pallas kernels  63.2 us (98%)
  between operations  0.66 us (1%)
    pallas_call x1, Pallas kernels, local(): pl.pallas_call(functools.partial(kernel, (nx, nz, nc, ny, nx * nz * nc *...  63.2 us

profile of v3, /device:TPU:1, one launch (start us, length us, event | category | flops | bytes accessed | tf_op | source)
XLA Modules:
  0.0 64.5 jit_solution(7642172940653719619)
XLA Ops:
  0.7 63.2 %shard_map.109 = bf16[64,64]{1,0:T(8,128)(2,1)S(1)} custom-call(s32[64]{0:T(128)} %len_hbm.1, s32[1]{0:T(128)S(6)} %copy.14.start_hbm, bf16[64,256]{1,0:T(8,128)(2,1)} %bitcast.7, bf16[1,64]{1,0:T(2,128)(2,1)} %g_hbm.1, bf16[64,1024]{1,0:T(8,128)(2,1)} %wq_hbm.1, bf16[64,256]{1,0:T(8,128)(2,1)} %wk_hbm.1, bf16[64,256]{1,0:T(8,128)(2,1)} %wv_hbm.1, ...), custom_call_target="tpu_custom_call" | custom-call | tf_op jit(solution)/shard_map/pallas_call | solution.py:728
  63.9 0.6 copy.13

commit v4 on v3

--- a/solution.py
+++ b/solution.py
@@ -18,6 +18,7 @@
 ROWS = 32
 CHUNK = 128
 KEYS = 512
+SMALL, BIG, WEIGHTS, LAST = range(4)
 
 rope_base = 500000.0
 stretch = 64.0
@@ -87,11 +88,9 @@
     ssc, sscr, ssx, ssxr, ssz, sszr, qbuf, s_ref,
     ob, lb, obs, obr, lss, lsr, oxs, oxr, lxs, lxr, wt,
     att, wobuf, p5s, p5r,
-    in_sem,
-    c1s, c1r, x1s, x1r, z1s, z1r, d1s, d1r, w1s, w1r, v1s, v1r, css, csr, xss, xsr, zss, zsr,
-    z2s, z2r, x2s, x2r, c2s, c2r, ws, wr, wcs, wcr,
-    c3s, c3r, c3ls, c3lr, x3s, x3r, x3ls, x3lr,
-    z4s, z4r, y5s, y5r,
+    dummy, in_sem, sent_sem,
+    c1r, x1r, z1r, d1r, w1r, v1r, csr, xsr, zsr,
+    z2r, x2r, c2r, wr, wcr, c3r, c3lr, x3r, x3lr, z4r, y5r,
 ):
     nx, nz, nc, ny, d_model = dims
     x, z, c, y = (lax.axis_index(n) for n in ("x", "z", "c", "y"))
@@ -109,10 +108,20 @@
     depth, span = h_ref.shape
     phase = Phases()
 
-    def copy(src, dst, send, recv, **to):
+    sent = [0, 0, 0, 0]
+
+    def copy(src, dst, kind, recv, **to):
         return pltpu.make_async_remote_copy(
-            src_ref=src, dst_ref=dst, send_sem=send, recv_sem=recv, device_id=to, device_id_type=MESH
+            src_ref=src, dst_ref=dst, send_sem=sent_sem.at[kind], recv_sem=recv,
+            device_id=to, device_id_type=MESH,
         )
+
+    def send(src, dst, kind, recv, **to):
+        copy(src, dst, kind, recv, **to).start()
+        sent[kind] += math.prod(src.shape) * jnp.dtype(src.dtype).itemsize
+
+    def receive(dst, recv):
+        copy(dst, dst, SMALL, recv, c=sib).wait_recv()
 
     def other_x(k):
         return lax.rem(x + k, nx)
@@ -194,11 +203,11 @@
     pl.semaphore_wait(barrier, jnp.where(x != y, peers + nc, peers))
 
     phase("core1_project")
-    core1 = [copy(sb.at[b], rb.at[b], c1s.at[b], c1r.at[b], c=sib) for b in range(nx)]
-    core2 = [copy(sb2.at[b], rb2.at[b], d1s.at[b], d1r.at[b], c=sib) for b in range(nx)]
-    sum_c = copy(ssc, sscr, css.at[0], csr.at[0], c=sib)
-    for one in (*core1, sum_c, *core2):
-        one.start()
+    for b in range(nx):
+        send(sb.at[b], rb.at[b], BIG, c1r, c=sib)
+    send(ssc, sscr, SMALL, csr, c=sib)
+    for b in range(nx):
+        send(sb2.at[b], rb2.at[b], BIG, d1r, c=sib)
 
     project(rows_of(c), (wq_ref,), own)
     project(rows_of(c), (wk_ref, wv_ref), own2)
@@ -206,17 +215,15 @@
     freq = freq_ref[...]
 
     phase("core1_wait")
-    for b in range(nx):
-        core1[b].wait_recv()
+    receive(rb, c1r)
     for k in x_far:
         b = other_x(k)
         xs[b] = (own[b] + rb[b].astype(F32)).astype(BF16)
-        copy(xs.at[b], xr.at[x], x1s.at[b], x1r.at[x], x=b).start()
-    sum_c.wait_recv()
+        send(xs.at[b], xr.at[x], BIG, x1r, x=b)
+    receive(sscr, csr)
     ssx[...] = ssc[...] + sscr[...]
     for k in x_far:
-        b = other_x(k)
-        copy(ssx, ssxr.at[x], xss.at[b], xsr.at[x], x=b).start()
+        send(ssx, ssxr.at[x], SMALL, xsr, x=other_x(k))
 
     phase("keys")
     get_len.wait()
@@ -282,31 +289,27 @@
 
     phase("x1_wait")
     gathered = own[x] + rb[x].astype(F32)
-    for k in x_near:
-        b = other_x(k)
-        copy(xs.at[b], xr.at[b], x1s.at[b], x1r.at[b], x=b).wait_recv()
-        gathered = gathered + xr[b].astype(F32)
+    receive(xr.at[pl.ds(0, nx - 1)], x1r)
+    for k in range(1, nx):
+        gathered = gathered + xr[other_x(k)].astype(F32)
     for t in range(nz):
         zs[t] = gathered[:, t * LANES : (t + 1) * LANES].astype(BF16)
     for k in z_far:
         b = other_z(k)
-        copy(zs.at[b], zr.at[z], z1s.at[b], z1r.at[z], z=b).start()
+        send(zs.at[b], zr.at[z], BIG, z1r, z=b)
     squares = ssx[...]
-    for k in x_near:
-        b = other_x(k)
-        copy(ssx, ssxr.at[b], xss.at[b], xsr.at[b], x=b).wait_recv()
-        squares = squares + ssxr[b]
+    receive(ssxr.at[pl.ds(0, nx - 1)], xsr)
+    for k in range(1, nx):
+        squares = squares + ssxr[other_x(k)]
     ssz[...] = squares
     for k in z_far:
-        b = other_z(k)
-        copy(ssz, sszr.at[z], zss.at[b], zsr.at[z], z=b).start()
-
-    for b in range(nx):
-        core2[b].wait_recv()
+        send(ssz, sszr.at[z], SMALL, zsr, z=other_z(k))
+
+    receive(rb2, d1r)
     for k in x_far:
         b = other_x(k)
         xs2[b] = (own2[b] + rb2[b].astype(F32)).astype(BF16)
-        copy(xs2.at[b], xr2.at[x], w1s.at[b], w1r.at[x], x=b).start()
+        send(xs2.at[b], xr2.at[x], BIG, w1r, x=b)
 
     phase("values")
     lax.fori_loop(early, steps, rotate_chunks, 0)
@@ -329,14 +332,12 @@
 
     phase("z1_wait")
     total = zs[z].astype(F32)
-    for k in z_near:
-        b = other_z(k)
-        copy(zs.at[b], zr.at[b], z1s.at[b], z1r.at[b], z=b).wait_recv()
-        total = total + zr[b].astype(F32)
-    for k in z_near:
-        b = other_z(k)
-        copy(ssz, sszr.at[b], zss.at[b], zsr.at[b], z=b).wait_recv()
-        squares = squares + sszr[b]
+    receive(zr.at[pl.ds(0, nz - 1)], z1r)
+    for k in range(1, nz):
+        total = total + zr[other_z(k)].astype(F32)
+    receive(sszr.at[pl.ds(0, nz - 1)], zsr)
+    for k in range(1, nz):
+        squares = squares + sszr[other_z(k)]
     wt[...] = as_columns(lax.rsqrt(squares * (1.0 / d_model) + epsilon))
     which = lax.div(first_token, LANES)
     lane = lax.rem(first_token, LANES)
@@ -352,22 +353,19 @@
     qbuf[c, x, z] = query.astype(BF16)
 
     for k in z_far:
-        b = other_z(k)
-        copy(qbuf.at[c, x, z], qbuf.at[c, x, z], z2s.at[b], z2r.at[z], z=b).start()
+        send(qbuf.at[c, x, z], qbuf.at[c, x, z], BIG, z2r.at[z], z=other_z(k))
 
     def piece_to_x(t):
         for k in x_far:
-            b = other_x(k)
-            copy(qbuf.at[c, x, t], qbuf.at[c, x, t], x2s.at[b, t], x2r.at[x, t], x=b).start()
+            send(qbuf.at[c, x, t], qbuf.at[c, x, t], BIG, x2r.at[x], x=other_x(k))
 
     piece_to_x(z)
 
     phase("new_keys")
     gathered = own2[x] + rb2[x].astype(F32)
-    for k in x_near:
-        b = other_x(k)
-        copy(xs2.at[b], xr2.at[b], w1s.at[b], w1r.at[b], x=b).wait_recv()
-        gathered = gathered + xr2[b].astype(F32)
+    receive(xr2.at[pl.ds(0, nx - 1)], w1r)
+    for k in range(1, nx):
+        gathered = gathered + xr2[other_x(k)].astype(F32)
     for t in range(nz):
         g, quarter = t // quarters, t % quarters
         pair = [
@@ -377,40 +375,24 @@
         zs2[t] = jnp.concatenate(pair, 0).astype(BF16)
     for k in z_far:
         b = other_z(k)
-        copy(zs2.at[b], zr2.at[z], v1s.at[b], v1r.at[z], z=b).start()
+        send(zs2.at[b], zr2.at[z], BIG, v1r, z=b)
 
     phase("z2_wait")
     for k in z_near:
         b = other_z(k)
-        copy(qbuf.at[c, x, b], qbuf.at[c, x, b], z2s.at[b], z2r.at[b], z=b).wait_recv()
+        receive(qbuf.at[c, x, b], z2r.at[b])
         piece_to_x(b)
 
-    phase("x2_wait")
-
     def block_to_core(b):
-        return copy(qbuf.at[c, b], qbuf.at[c, b], c2s.at[b], c2r.at[b], c=sib)
-
-    block_to_core(x).start()
-    for k in x_near:
-        b = other_x(k)
-        for t in range(nz):
-            copy(qbuf.at[c, b, t], qbuf.at[c, b, t], x2s.at[b, t], x2r.at[b, t], x=b).wait_recv()
-        block_to_core(b).start()
-    for k in x_far:
-        b = other_x(k)
-        copy(wobuf.at[x, c], wobuf.at[x, c], ws.at[b], wr.at[x], x=b).start()
-
-    def weights_to_core(b):
-        return copy(wobuf.at[b, c], wobuf.at[b, c], wcs.at[b], wcr.at[b], c=sib)
-
-    weights_to_core(x).start()
+        send(qbuf.at[c, b], qbuf.at[c, b], BIG, c2r.at[b], c=sib)
+
+    block_to_core(x)
 
     phase("new_keys_wait")
     total = zs2[z].astype(F32)
-    for k in z_near:
-        b = other_z(k)
-        copy(zs2.at[b], zr2.at[b], v1s.at[b], v1r.at[b], z=b).wait_recv()
-        total = total + zr2[b].astype(F32)
+    receive(zr2.at[pl.ds(0, nz - 1)], v1r)
+    for k in range(1, nz):
+        total = total + zr2[other_z(k)].astype(F32)
     inv_new = inverse_of(lane + my_quarter * tail, tail)
     new_k = (total[0:tail] * inv_new).astype(BF16).astype(F32)
     new_k = rotated(new_k, k_cos, k_sin)
@@ -424,20 +406,22 @@
         vs[g, slots:, 0:LANES] = new_v
         vs[g, slots:, LANES:] = new_ones
 
-    rows = 2 * block
-    apart = nx // 2
-    pairs = [(i, i + apart) for i in range(apart)]
-
-    def attend(cc, pair):
-        blocks = [other_x(k) for k in pair]
-        row = iota((rows, LANES), 0)
-        token = jnp.where(row < block, blocks[0], blocks[1]) * per_x + cc * ROWS + lax.rem(row, ROWS)
+    def attend(blocks):
+        rows = len(blocks) * block
+        token = jnp.concatenate(
+            [
+                other_x(k) * per_x + cc * ROWS + lax.rem(iota((block, LANES), 0), ROWS)
+                for cc, k in blocks
+            ],
+            0,
+        )
         lane = iota((rows, LANES), 1)
         seen = jnp.logical_and(lane < tail, k_first + lane <= token)
         for g in range(kv):
-            q = jnp.concatenate(
-                [qbuf[cc, b, g * group : (g + 1) * group].reshape(block, LANES) for b in blocks], 0
-            )
+            q = [
+                qbuf[cc, other_x(k), g * group : (g + 1) * group].reshape(block, LANES) for cc, k in blocks
+            ]
+            q = jnp.concatenate(q, 0)
             most = jnp.full((rows, LANES), negative, F32)
             for at in range(0, slots, KEYS):
                 score = lax.dot_general(
@@ -460,106 +444,94 @@
             sums = acc[:, LANES:]
             result = acc[:, 0:LANES] / sums
             lse = most + jnp.log(sums)
-            for j, b in enumerate(blocks):
-                cut = slice(j * block, (j + 1) * block)
-                yield b, g, result[cut], lse[cut].T[0:1]
-
-    def core3(b):
-        return (
-            copy(obs.at[b], obr.at[b], c3s.at[b], c3r.at[b], c=sib),
-            copy(lss.at[b], lsr.at[b], c3ls.at[b], c3lr.at[b], c=sib),
-        )
-
-    def combine(outs, logs):
-        top = functools.reduce(jnp.maximum, logs)
-        weights = [jnp.exp(v - top) for v in logs]
-        whole = sum(weights)
-        spare = jnp.zeros((8 - kv, LANES), F32)
-        columns = as_columns(
-            jnp.concatenate([jnp.concatenate([w / whole, spare], 0) for w in weights], 0)
-        )
-        parts = []
-        for g in range(kv):
-            cut = slice(g * block, (g + 1) * block)
-            parts.append(sum(columns[:, 8 * i + g : 8 * i + g + 1] * o[cut] for i, o in enumerate(outs)))
-        return jnp.concatenate(parts, 0), top + jnp.log(whole)
-
-    def own_unit(pair):
-        for b, g, result, lse in attend(c, pair):
-            ob[b, g * block : (g + 1) * block, :] = result
-            lb[b, g : g + 1, :] = lse
-
-    def sibling_unit(pair):
-        for b, g, result, lse in attend(sib, pair):
-            obs[b, g * block : (g + 1) * block, :] = result.astype(BF16)
-            lss[b, g : g + 1, :] = lse
-        for k in pair:
-            for one in core3(other_x(k)):
-                one.start()
+            for j, (cc, k) in enumerate(blocks):
+                b, cut = other_x(k), slice(j * block, (j + 1) * block)
+                if cc is sib:
+                    obs[b, g * block : (g + 1) * block, :] = result[cut].astype(BF16)
+                    lss[b, g : g + 1, :] = lse[cut].T[0:1]
+                else:
+                    ob[b, g * block : (g + 1) * block, :] = result[cut]
+                    lb[b, g : g + 1, :] = lse[cut].T[0:1]
+        for cc, k in blocks:
+            if cc is sib:
+                b = other_x(k)
+                send(obs.at[b], obr.at[b], BIG, c3r.at[b], c=sib)
+                send(lss.at[b], lsr.at[b], SMALL, c3lr.at[b], c=sib)
 
     away = sorted(
         ((i, j) for i in range(nx) for j in range(nz)),
         key=lambda k: -min(k[0], nx - k[0]) - min(k[1], nz - k[1]),
     )
 
-    def piece3(i, j):
-        b, t = other_x(i), other_z(j)
-        return (
-            copy(oxs.at[b, t], oxr.at[x, z], x3s.at[b, t], x3r.at[x, z], x=b, z=t),
-            copy(lxs.at[b], lxr.at[x, z], x3ls.at[b, t], x3lr.at[x, z], x=b, z=t),
-        )
-
-    def arrival3(i, j):
-        b, t = other_x(i), other_z(j)
-        return (
-            copy(oxs.at[b, t], oxr.at[b, t], x3s.at[b, t], x3r.at[b, t], x=b, z=t),
-            copy(lxs.at[b], lxr.at[b, t], x3ls.at[b, t], x3lr.at[b, t], x=b, z=t),
-        )
-
-    def join_cores(pair):
-        for k in pair:
-            b = other_x(k)
-            for one in core3(b):
-                one.wait_recv()
-            out, lse = combine([ob[b], obr[b].astype(F32)], [lb[b], lsr[b]])
-            oxs[b] = out.astype(BF16).reshape(nz, ROWS, LANES)
+    def join(places):
+        weights, blocks = [], [other_x(k) for k in places]
+        for b in blocks:
+            receive(obr.at[b], c3r.at[b])
+            receive(lsr.at[b], c3lr.at[b])
+            logs = [lb[b], lsr[b]]
+            top = jnp.maximum(*logs)
+            lse = top + jnp.log(sum(jnp.exp(v - top) for v in logs))
+            weights += [jnp.exp(v - lse) for v in logs]
             lxs[b] = lse
+        columns = as_columns(jnp.concatenate(weights, 0))
+        for i, b in enumerate(blocks):
+            for g in range(kv):
+                cut = slice(g * block, (g + 1) * block)
+                at = 2 * kv * i + g
+                out = columns[:, at : at + 1] * ob[b, cut, :]
+                out = out + columns[:, at + kv : at + kv + 1] * obr[b, cut, :].astype(F32)
+                oxs[b, g * group : (g + 1) * group] = out.astype(BF16).reshape(group, ROWS, LANES)
         for i, j in away:
-            if i in pair and (i or j):
-                for one in piece3(i, j):
-                    one.start()
-
+            if i in places and (i or j):
+                b, t = other_x(i), other_z(j)
+                send(oxs.at[b, t], oxr.at[x * nz + z], BIG, x3r, x=b, z=t)
+                send(lxs.at[b], lxr.at[x * nz + z], SMALL, x3lr, x=b, z=t)
+
+    middle, final_x = list(range(1, nx - 1)), nx - 1
+    phase("c2_wait")
+    receive(qbuf.at[sib, x], c2r.at[x])
     phase("unit_0")
-    own_unit(pairs[0])
-    phase("c2_wait")
-    for k in range(nx):
+    attend([(c, 0), (sib, 0)])
+    phase("x2_wait")
+    for k in x_near:
         b = other_x(k)
-        copy(qbuf.at[sib, b], qbuf.at[sib, b], c2s.at[b], c2r.at[b], c=sib).wait_recv()
-    for i, pair in enumerate(pairs):
+        receive(qbuf.at[c, b], x2r.at[b])
+        block_to_core(b)
+    for k in x_far:
+        send(wobuf.at[x, c], wobuf.at[x, c], WEIGHTS, wr, x=other_x(k))
+    send(wobuf.at[x, c], wobuf.at[x, c], WEIGHTS, wcr, c=sib)
+    if middle:
         phase("unit_1")
-        sibling_unit(pair)
-        if i == 0:
-            phase("weights")
-            for k in x_near:
-                b = other_x(k)
-                copy(wobuf.at[b, c], wobuf.at[b, c], ws.at[b], wr.at[b], x=b).wait_recv()
-                weights_to_core(b).start()
-    phase("join")
-    join_cores(pairs[0])
-    for pair in pairs[1:]:
+        attend([(c, k) for k in middle])
+        phase("c2_wait2")
+        for k in middle:
+            receive(qbuf.at[sib, other_x(k)], c2r.at[other_x(k)])
         phase("unit_2")
-        own_unit(pair)
-        phase("join_2")
-        join_cores(pair)
+        attend([(sib, k) for k in middle])
+    phase("join_0")
+    join([0])
+    if middle:
+        phase("join_1")
+        join(middle)
+    receive(qbuf.at[sib, other_x(final_x)], c2r.at[other_x(final_x)])
+    phase("unit_3")
+    attend([(sib, final_x), (c, final_x)])
+    phase("join_3")
+    join([final_x])
+    receive(wobuf.at[pl.ds(0, nx - 1), c], wr)
+    for k in range(1, nx):
+        b = other_x(k)
+        send(wobuf.at[b, c], wobuf.at[b, c], WEIGHTS, wcr, c=sib)
 
     phase("x3_wait")
     outs, logs = [oxs[x, z]], [lxs[x]]
-    for i, j in away[::-1]:
+    receive(oxr.at[pl.ds(0, nx * nz - 1)], x3r)
+    receive(lxr.at[pl.ds(0, nx * nz - 1)], x3lr)
+    for i, j in away:
         if i or j:
-            for one in arrival3(i, j):
-                one.wait_recv()
-            outs.append(oxr[other_x(i), other_z(j)])
-            logs.append(lxr[other_x(i), other_z(j)])
+            at = other_x(i) * nz + other_z(j)
+            outs.append(oxr[at])
+            logs.append(lxr[at])
     phase("combine")
     picked = []
     for v in logs:
@@ -575,17 +547,11 @@
     att[z] = attended.astype(BF16)
 
     for k in z_far:
-        b = other_z(k)
-        copy(att.at[z], att.at[z], z4s.at[b], z4r.at[z], z=b).start()
+        send(att.at[z], att.at[z], BIG, z4r, z=other_z(k))
 
     phase("z4_wait")
-    for k in range(1, nx):
-        b = other_x(k)
-        copy(wobuf.at[b, sib], wobuf.at[b, sib], wcs.at[b], wcr.at[b], c=sib).wait_recv()
-    copy(wobuf.at[x, sib], wobuf.at[x, sib], wcs.at[x], wcr.at[x], c=sib).wait_recv()
-    for k in z_near:
-        b = other_z(k)
-        copy(att.at[b], att.at[b], z4s.at[b], z4r.at[b], z=b).wait_recv()
+    receive(wobuf.at[:, sib], wcr)
+    receive(att.at[pl.ds(0, nz - 1)], z4r)
 
     phase("w_out")
     lhs = jnp.concatenate([att[t] for t in range(heads)], 1)
@@ -599,77 +565,57 @@
         p5s[b, 0] = jnp.where(low, both[0:deep], turned[deep:]).astype(BF16)
         p5s[b, 1] = jnp.where(low, turned[0:deep], both[deep:]).astype(BF16)
 
+    me = c * ny + y
+
     def last(b, cc):
-        return copy(p5s.at[b, cc], p5r.at[c, y], y5s.at[b, cc], y5r.at[c, y], x=b, c=cc, y=x)
+        copy(p5s.at[b, cc], p5r.at[me], LAST, y5r, x=b, c=cc, y=x).start()
 
     for k in x_far:
         for cc in range(nc):
-            last(other_x(k), cc).start()
-    last(x, sib).start()
+            last(other_x(k), cc)
+    last(x, sib)
 
     @pl.when(x != y)
     def _():
-        last(x, c).start()
+        last(x, c)
 
     @pl.when(x == y)
     def _():
-        p5r[c, y] = p5s[x, c]
+        p5r[me] = p5s[x, c]
 
     phase("y5_wait")
-
-    def arrival(cc, b):
-        return copy(p5s.at[y, cc], p5r.at[cc, b], y5s.at[y, cc], y5r.at[cc, b], x=y, c=cc, y=b)
-
-    for k in range(1, ny):
-        for cc in range(nc):
-            arrival(cc, lax.rem(y + k, ny)).wait_recv()
-    arrival(sib, y).wait_recv()
 
     @pl.when(x != y)
     def _():
-        arrival(c, y).wait_recv()
+        receive(p5r, y5r)
+
+    @pl.when(x == y)
+    def _():
+        receive(p5r.at[pl.ds(0, nc * ny - 1)], y5r)
 
     for cc in range(nc):
-        final = sum(p5r[cc, b].astype(F32) for b in range(ny))
+        final = sum(p5r[cc * ny + b].astype(F32) for b in range(ny))
         at = cc * ROWS
         out_ref[at : at + deep, :] = final[:, 0:HALF].astype(BF16)
         out_ref[at + deep : at + ROWS, :] = pltpu.roll(final, HALF, 1)[:, 0:HALF].astype(BF16)
 
     phase("drain")
-    sum_c.wait_send()
-    for b in range(nx):
-        core1[b].wait_send()
-        core2[b].wait_send()
-        block_to_core(b).wait_send()
-        weights_to_core(b).wait_send()
-        for one in core3(b):
-            one.wait_send()
-    for k in range(1, nx):
-        b = other_x(k)
-        copy(xs.at[b], xr.at[x], x1s.at[b], x1r.at[x], x=b).wait_send()
-        copy(ssx, ssxr.at[x], xss.at[b], xsr.at[x], x=b).wait_send()
-        copy(wobuf.at[x, c], wobuf.at[x, c], ws.at[b], wr.at[x], x=b).wait_send()
-        for t in range(nz):
-            copy(qbuf.at[c, x, t], qbuf.at[c, x, t], x2s.at[b, t], x2r.at[x, t], x=b).wait_send()
-        copy(xs2.at[b], xr2.at[x], w1s.at[b], w1r.at[x], x=b).wait_send()
-        for cc in range(nc):
-            last(b, cc).wait_send()
-    for k in range(1, nz):
-        b = other_z(k)
-        copy(zs.at[b], zr.at[z], z1s.at[b], z1r.at[z], z=b).wait_send()
-        copy(ssz, sszr.at[z], zss.at[b], zsr.at[z], z=b).wait_send()
-        copy(qbuf.at[c, x, z], qbuf.at[c, x, z], z2s.at[b], z2r.at[z], z=b).wait_send()
-        copy(zs2.at[b], zr2.at[z], v1s.at[b], v1r.at[z], z=b).wait_send()
-        copy(att.at[z], att.at[z], z4s.at[b], z4r.at[z], z=b).wait_send()
-    last(x, sib).wait_send()
-    for i, j in away:
-        if i or j:
-            for one in piece3(i, j):
-                one.wait_send()
+
+    def gone(ref, kind):
+        copy(ref, ref, kind, c1r, c=sib).wait_send()
+
+    line = LANES * jnp.dtype(BF16).itemsize
+    gone(dummy.at[pl.ds(0, sent[SMALL] // (2 * line))], SMALL)
+    gone(kraw.at[pl.ds(0, sent[BIG] // line)], BIG)
+    gone(kraw.at[pl.ds(0, sent[WEIGHTS] // line)], WEIGHTS)
 
     @pl.when(x != y)
     def _():
-        last(x, c).wait_send()
+        gone(p5r, LAST)
+
+    @pl.when(x == y)
+    def _():
+        gone(p5r.at[pl.ds(0, nc * ny - 1)], LAST)
 
     phase(None)
 
@@ -710,20 +656,14 @@
         V((nc, nx, heads, ROWS, LANES), BF16), V((kv, rows, slots), F32),
         V((nx, block, LANES), F32), V((nx, kv, LANES), F32),
         V((nx, block, LANES), BF16), V((nx, block, LANES), BF16), V((nx, kv, LANES), F32), V((nx, kv, LANES), F32),
-        V((nx, nz, ROWS, LANES), BF16), V((nx, nz, ROWS, LANES), BF16),
-        V((nx, kv, LANES), F32), V((nx, nz, kv, LANES), F32),
+        V((nx, nz, ROWS, LANES), BF16), V((nx * nz, ROWS, LANES), BF16),
+        V((nx, kv, LANES), F32), V((nx * nz, kv, LANES), F32),
         V((LANES, LANES), F32),
         V((heads, ROWS, LANES), BF16), V((nx, nc, HALF, w_out.shape[0]), BF16),
-        V((nx, nc, ROWS // 2, LANES), BF16), V((nc, ny, ROWS // 2, LANES), BF16),
-        dma((11,)),
-        dma((nx,)), dma((nx,)), dma((nx,)), dma((nx,)), dma((nz,)), dma((nz,)),
-        dma((nx,)), dma((nx,)), dma((nx,)), dma((nx,)), dma((nz,)), dma((nz,)),
-        dma((1,)), dma((1,)), dma((nx,)), dma((nx,)), dma((nz,)), dma((nz,)),
-        dma((nz,)), dma((nz,)), dma((nx, nz)), dma((nx, nz)), dma((nx,)), dma((nx,)),
-        dma((nx,)), dma((nx,)), dma((nx,)), dma((nx,)),
-        dma((nx,)), dma((nx,)), dma((nx,)), dma((nx,)),
-        dma((nx, nz)), dma((nx, nz)), dma((nx, nz)), dma((nx, nz)),
-        dma((nz,)), dma((nz,)), dma((nx, nc)), dma((nc, ny)),
+        V((nx, nc, ROWS // 2, LANES), BF16), V((nc * ny, ROWS // 2, LANES), BF16),
+        V((128, 1, LANES), F32), dma((11,)), dma((4,)),
+        dma, dma, dma, dma, dma, dma, dma, dma, dma,
+        dma((nz,)), dma((nx,)), dma((nx,)), dma, dma, dma((nx,)), dma((nx,)), dma, dma, dma, dma,
     ]
     return pl.pallas_call(
         functools.partial(kernel, (nx, nz, nc, ny, nx * nz * nc * depth)),

time: 64.6 us -> 58.7 us (0.909)
  Pallas kernels: 63.2 us -> 57.4 us
    pallas_call x1, Pallas kernels: 63.2 us -> 57.4 us  [local(): pl.pallas_call(functools.partial(kernel, (nx, nz, nc, ny, nx * nz * nc *...]
where the time goes in v4:
time: 58.7 us; the launch traced here: 58.6 us
  Pallas kernels  57.4 us (98%)
  between operations  0.66 us (1%)
  local copies, waits for them, and re-layouts  0.61 us (1%)
    pallas_call x1, Pallas kernels, local(): pl.pallas_call(functools.partial(kernel, (nx, nz, nc, ny, nx * nz * nc *...  57.4 us

profile of v4, /device:TPU:1, one launch (start us, length us, event | category | flops | bytes accessed | tf_op | source)
XLA Modules:
  0.0 58.6 jit_solution(1044158289626218898)
XLA Ops:
  0.7 57.4 %shard_map.109 = bf16[64,64]{1,0:T(8,128)(2,1)S(1)} custom-call(s32[64]{0:T(128)} %len_hbm.1, s32[1]{0:T(128)S(6)} %copy.14.start_hbm, bf16[64,256]{1,0:T(8,128)(2,1)} %bitcast.7, bf16[1,64]{1,0:T(2,128)(2,1)} %g_hbm.1, bf16[64,1024]{1,0:T(8,128)(2,1)} %wq_hbm.1, bf16[64,256]{1,0:T(8,128)(2,1)} %wk_hbm.1, bf16[64,256]{1,0:T(8,128)(2,1)} %wv_hbm.1, ...), custom_call_target="tpu_custom_call" | custom-call | tf_op jit(solution)/shard_map/pallas_call | solution.py:668
  58.0 0.6 %copy.13 = bf16[64,64]{1,0:T(8,128)(2,1)} copy(bf16[64,64]{1,0:T(8,128)(2,1)S(1)} %shard_map.109) | data formatting | bytes 16384

commit v5 on v4

--- a/solution.py
+++ b/solution.py
@@ -89,7 +89,7 @@
     ob, lb, obs, obr, lss, lsr, oxs, oxr, lxs, lxr, wt,
     att, wobuf, p5s, p5r,
     dummy, in_sem, sent_sem,
-    c1r, x1r, z1r, d1r, w1r, v1r, csr, xsr, zsr,
+    hear_x, hear_z, hear_y, rel, merged, relr, c1r, x1r, z1r, d1r, w1r, v1r, csr, xsr, zsr,
     z2r, x2r, c2r, wr, wcr, c3r, c3lr, x3r, x3lr, z4r, y5r,
 ):
     nx, nz, nc, ny, d_model = dims
@@ -106,6 +106,7 @@
     per_x = nc * ROWS
     block = group * ROWS
     depth, span = h_ref.shape
+    cols = own.shape[2]
     phase = Phases()
 
     sent = [0, 0, 0, 0]
@@ -140,20 +141,24 @@
     def greet(**to):
         pl.semaphore_signal(barrier, inc=1, device_id=to, device_id_type=MESH)
 
-    for k in z_far:
-        greet(z=other_z(k))
-    for k in range(1, ny):
-        for cc in range(nc):
-            greet(x=y, y=lax.rem(y + k, ny), c=cc)
-
-    @pl.when(x != y)
-    def _():
-        for cc in range(nc):
-            greet(x=y, c=cc)
-
-    for k in x_far:
-        greet(x=other_x(k))
+    beside = {"x": sorted({1, nx - 1}), "z": sorted({1, nz - 1}), "y": sorted({1, ny - 1})}
+    places = {"x": (x, nx), "z": (z, nz), "y": (y, ny)}
+
+    def neighbours(axis):
+        at, size = places[axis]
+        return [{axis: lax.rem(at + k, size)} for k in beside[axis]]
+
+    for axis in ("z", "x", "y"):
+        for to in neighbours(axis):
+            greet(**to)
     greet(c=sib)
+
+    def tell(sem, axis):
+        for to in neighbours(axis):
+            pl.semaphore_signal(sem, inc=1, device_id=to, device_id_type=MESH)
+
+    def hear(sem, axis):
+        pl.semaphore_wait(sem, len(beside[axis]))
 
     fetches = []
     for i, (src, dst) in enumerate(
@@ -199,8 +204,9 @@
     project(rows_of(sib), (wk_ref, wv_ref), sb2)
 
     phase("barrier")
-    peers = 1 + (nx - 1) + (nz - 1) + nc * (ny - 1)
-    pl.semaphore_wait(barrier, jnp.where(x != y, peers + nc, peers))
+    pl.semaphore_wait(barrier, 1 + sum(len(beside[axis]) for axis in beside))
+    tell(hear_x, "x")
+    tell(hear_z.at[0], "z")
 
     phase("core1_project")
     for b in range(nx):
@@ -216,10 +222,31 @@
 
     phase("core1_wait")
     receive(rb, c1r)
+    hear(hear_x, "x")
+    hear(hear_z.at[0], "z")
+    tell(hear_z.at[1], "z")
+    relayed = nx == 4
+    deep = ROWS // 2
     for k in x_far:
         b = other_x(k)
-        xs[b] = (own[b] + rb[b].astype(F32)).astype(BF16)
-        send(xs.at[b], xr.at[x], BIG, x1r, x=b)
+        sums = (own[b] + rb[b].astype(F32)).astype(BF16)
+        xs[2 * b] = sums[0:deep]
+        xs[2 * b + 1] = sums[deep:]
+        send(xs.at[2 * b], xr.at[2 * x], BIG, x1r, x=b)
+        if relayed and k > 1:
+            def direct():
+                copy(xs.at[2 * b + 1], xr.at[2 * x + 1], BIG, x1r, x=b).start()
+
+            pl.when(c == 0)(direct)
+            if k == 2:
+
+                @pl.when(c == 1)
+                def _():
+                    copy(xs.at[2 * b + 1], rel, BIG, relr, x=other_x(3)).start()
+
+            sent[BIG] += deep * cols * 2
+        else:
+            send(xs.at[2 * b + 1], xr.at[2 * x + 1], BIG, x1r, x=b)
     receive(sscr, csr)
     ssx[...] = ssc[...] + sscr[...]
     for k in x_far:
@@ -288,10 +315,33 @@
     lax.fori_loop(0, early, rotate_chunks, 0)
 
     phase("x1_wait")
+    hear(hear_z.at[1], "z")
+    tell(hear_z.at[2], "z")
     gathered = own[x] + rb[x].astype(F32)
-    receive(xr.at[pl.ds(0, nx - 1)], x1r)
+    if relayed:
+
+        @pl.when(c == 1)
+        def _():
+            b = other_x(3)
+            receive(rel, relr)
+            merged[...] = (own[b, deep:] + rb[b, deep:].astype(F32) + rel[...].astype(F32)).astype(BF16)
+            copy(merged, xr.at[2 * x + 1], BIG, x1r, x=b).start()
+            receive(xr.at[pl.ds(0, 2 * nx - 3)], x1r)
+
+        @pl.when(c == 0)
+        def _():
+            receive(xr.at[pl.ds(0, 2 * nx - 2)], x1r)
+
+    else:
+        receive(xr.at[pl.ds(0, 2 * nx - 2)], x1r)
     for k in range(1, nx):
-        gathered = gathered + xr[other_x(k)].astype(F32)
+        b = other_x(k)
+        second = xr[2 * b + 1].astype(F32)
+        if relayed and k == 2:
+            second = jnp.where(c == 0, second, 0.0)
+        gathered = gathered + jnp.concatenate([xr[2 * b].astype(F32), second], 0)
+    tell(hear_y.at[0], "y")
+    hear(hear_z.at[2], "z")
     for t in range(nz):
         zs[t] = gathered[:, t * LANES : (t + 1) * LANES].astype(BF16)
     for k in z_far:
@@ -330,38 +380,7 @@
     lax.fori_loop(0, steps, value_chunks, 0)
     get_wo.wait()
 
-    phase("z1_wait")
-    total = zs[z].astype(F32)
-    receive(zr.at[pl.ds(0, nz - 1)], z1r)
-    for k in range(1, nz):
-        total = total + zr[other_z(k)].astype(F32)
-    receive(sszr.at[pl.ds(0, nz - 1)], zsr)
-    for k in range(1, nz):
-        squares = squares + sszr[other_z(k)]
-    wt[...] = as_columns(lax.rsqrt(squares * (1.0 / d_model) + epsilon))
-    which = lax.div(first_token, LANES)
-    lane = lax.rem(first_token, LANES)
-
-    def inverse_of(at, size):
-        cols = wt[pl.ds(pl.multiple_of(at, 8), size), :]
-        picked = cols[:, 0:1]
-        for r in range(1, span // LANES):
-            picked = jnp.where(which == r, cols[:, r : r + 1], picked)
-        return picked
-
-    query = rotated(total * inverse_of(lane, ROWS), q_cos, q_sin) * LANES**-0.5
-    qbuf[c, x, z] = query.astype(BF16)
-
-    for k in z_far:
-        send(qbuf.at[c, x, z], qbuf.at[c, x, z], BIG, z2r.at[z], z=other_z(k))
-
-    def piece_to_x(t):
-        for k in x_far:
-            send(qbuf.at[c, x, t], qbuf.at[c, x, t], BIG, x2r.at[x], x=other_x(k))
-
-    piece_to_x(z)
-
-    phase("new_keys")
+    phase("kv_pieces")
     gathered = own2[x] + rb2[x].astype(F32)
     receive(xr2.at[pl.ds(0, nx - 1)], w1r)
     for k in range(1, nx):
@@ -377,6 +396,46 @@
         b = other_z(k)
         send(zs2.at[b], zr2.at[z], BIG, v1r, z=b)
 
+    phase("z1_wait")
+    hear(hear_y.at[0], "y")
+    tell(hear_y.at[1], "y")
+    total = zs[z].astype(F32)
+    receive(zr.at[pl.ds(0, nz - 1)], z1r)
+    for k in range(1, nz):
+        total = total + zr[other_z(k)].astype(F32)
+    receive(sszr.at[pl.ds(0, nz - 1)], zsr)
+    for k in range(1, nz):
+        squares = squares + sszr[other_z(k)]
+    wt[...] = as_columns(lax.rsqrt(squares * (1.0 / d_model) + epsilon))
+    which = lax.div(first_token, LANES)
+    lane = lax.rem(first_token, LANES)
+
+    def inverse_of(at, size):
+        cols = wt[pl.ds(pl.multiple_of(at, 8), size), :]
+        picked = cols[:, 0:1]
+        for r in range(1, span // LANES):
+            picked = jnp.where(which == r, cols[:, r : r + 1], picked)
+        return picked
+
+    query = rotated(total * inverse_of(lane, ROWS), q_cos, q_sin) * LANES**-0.5
+    qbuf[c, x, z] = query.astype(BF16)
+
+    for k in z_far:
+        send(qbuf.at[c, x, z], qbuf.at[c, x, z], BIG, z2r.at[z], z=other_z(k))
+
+    @pl.when(c == 0)
+    def _():
+        mine = qbuf.at[c, x, z]
+        for k in z_far:
+            copy(mine, mine, BIG, c2r.at[x], z=other_z(k), c=1).start()
+        copy(mine, mine, BIG, c2r.at[x], c=1).start()
+
+    def piece_to_x(t):
+        for k in x_far:
+            send(qbuf.at[c, x, t], qbuf.at[c, x, t], BIG, x2r.at[x], x=other_x(k))
+
+    piece_to_x(z)
+
     phase("z2_wait")
     for k in z_near:
         b = other_z(k)
@@ -386,7 +445,11 @@
     def block_to_core(b):
         send(qbuf.at[c, b], qbuf.at[c, b], BIG, c2r.at[b], c=sib)
 
-    block_to_core(x)
+    @pl.when(c == 1)
+    def _():
+        copy(qbuf.at[c, x], qbuf.at[c, x], BIG, c2r.at[x], c=sib).start()
+
+    sent[BIG] += heads * ROWS * LANES * 2
 
     phase("new_keys_wait")
     total = zs2[z].astype(F32)
@@ -557,7 +620,6 @@
     lhs = jnp.concatenate([att[t] for t in range(heads)], 1)
     rhs = wobuf[...].reshape(nx * nc * HALF, heads * LANES)
     got = lax.dot_general(lhs, rhs, (((1,), (1,)), ((), ())), preferred_element_type=F32)
-    deep = ROWS // 2
     low = iota((deep, LANES), 1) < HALF
     for b in range(nx):
         both = got[:, b * LANES : (b + 1) * LANES]
@@ -566,6 +628,7 @@
         p5s[b, 1] = jnp.where(low, turned[0:deep], both[deep:]).astype(BF16)
 
     me = c * ny + y
+    hear(hear_y.at[1], "y")
 
     def last(b, cc):
         copy(p5s.at[b, cc], p5r.at[me], LAST, y5r, x=b, c=cc, y=x).start()
@@ -646,7 +709,7 @@
         V((kv, keys, LANES), BF16), V((kv, keys, 2 * LANES), BF16),
         V((2, slots // CHUNK, LANES), F32), V((2, CHUNK, LANES), F32),
         V((nx, ROWS, cols), BF16), V((nx, ROWS, cols), BF16), V((nx, ROWS, cols), F32),
-        V((nx, ROWS, cols), BF16), V((nx, ROWS, cols), BF16),
+        V((2 * nx, ROWS // 2, cols), BF16), V((2 * nx, ROWS // 2, cols), BF16),
         V((nz, ROWS, LANES), BF16), V((nz, ROWS, LANES), BF16),
         V((nx, ROWS, cols2), BF16), V((nx, ROWS, cols2), BF16), V((nx, ROWS, cols2), F32),
         V((nx, ROWS, cols2), BF16), V((nx, ROWS, cols2), BF16),
@@ -662,7 +725,9 @@
         V((heads, ROWS, LANES), BF16), V((nx, nc, HALF, w_out.shape[0]), BF16),
         V((nx, nc, ROWS // 2, LANES), BF16), V((nc * ny, ROWS // 2, LANES), BF16),
         V((128, 1, LANES), F32), dma((11,)), dma((4,)),
-        dma, dma, dma, dma, dma, dma, dma, dma, dma,
+        pltpu.SemaphoreType.REGULAR, pltpu.SemaphoreType.REGULAR((3,)), pltpu.SemaphoreType.REGULAR((2,)),
+        V((ROWS // 2, cols), BF16), V((ROWS // 2, cols), BF16),
+        dma, dma, dma, dma, dma, dma, dma, dma, dma, dma,
         dma((nz,)), dma((nx,)), dma((nx,)), dma, dma, dma((nx,)), dma((nx,)), dma, dma, dma, dma,
     ]
     return pl.pallas_call(

time: 58.7 us -> 57.3 us (0.976)
  Pallas kernels: 57.4 us -> 55.9 us
    pallas_call x1, Pallas kernels: 57.4 us -> 55.9 us  [local(): pl.pallas_call(functools.partial(kernel, (nx, nz, nc, ny, nx * nz * nc *...]
where the time goes in v5:
time: 57.3 us; the launch traced here: 57.2 us
  Pallas kernels  55.9 us (98%)
  between operations  0.66 us (1%)
  local copies, waits for them, and re-layouts  0.61 us (1%)
    pallas_call x1, Pallas kernels, local(): pl.pallas_call(functools.partial(kernel, (nx, nz, nc, ny, nx * nz * nc *...  55.9 us

profile of v5, /device:TPU:1, one launch (start us, length us, event | category | flops | bytes accessed | tf_op | source)
XLA Modules:
  0.0 57.2 jit_solution(9402377513174231431)
XLA Ops:
  0.7 55.9 %shard_map.109 = bf16[64,64]{1,0:T(8,128)(2,1)S(1)} custom-call(s32[64]{0:T(128)} %len_hbm.1, s32[1]{0:T(128)S(6)} %copy.14.start_hbm, bf16[64,256]{1,0:T(8,128)(2,1)} %bitcast.7, bf16[1,64]{1,0:T(2,128)(2,1)} %g_hbm.1, bf16[64,1024]{1,0:T(8,128)(2,1)} %wq_hbm.1, bf16[64,256]{1,0:T(8,128)(2,1)} %wk_hbm.1, bf16[64,256]{1,0:T(8,128)(2,1)} %wv_hbm.1, ...), custom_call_target="tpu_custom_call" | custom-call | tf_op jit(solution)/shard_map/pallas_call | solution.py:733
  56.6 0.6 %copy.13 = bf16[64,64]{1,0:T(8,128)(2,1)} copy(bf16[64,64]{1,0:T(8,128)(2,1)S(1)} %shard_map.109) | data formatting | bytes 16384

commit v6 on v5

--- a/solution.py
+++ b/solution.py
@@ -544,11 +544,23 @@
                 out = columns[:, at : at + 1] * ob[b, cut, :]
                 out = out + columns[:, at + kv : at + kv + 1] * obr[b, cut, :].astype(F32)
                 oxs[b, g * group : (g + 1) * group] = out.astype(BF16).reshape(group, ROWS, LANES)
+        slot = c * nx * nz + x * nz + z
         for i, j in away:
             if i in places and (i or j):
                 b, t = other_x(i), other_z(j)
-                send(oxs.at[b, t], oxr.at[x * nz + z], BIG, x3r, x=b, z=t)
-                send(lxs.at[b], lxr.at[x * nz + z], SMALL, x3lr, x=b, z=t)
+                send(oxs.at[b, t], oxr.at[slot], BIG, x3r, x=b, z=t, c=1)
+                send(lxs.at[b], lxr.at[slot], SMALL, x3lr, x=b, z=t, c=1)
+        if 0 in places:
+
+            @pl.when(c == 0)
+            def _():
+                copy(oxs.at[x, z], oxr.at[slot], BIG, x3r, c=1).start()
+                copy(lxs.at[x], lxr.at[slot], SMALL, x3lr, c=1).start()
+
+            @pl.when(c == 1)
+            def _():
+                oxr[slot] = oxs[x, z]
+                lxr[slot] = lxs[x]
 
     middle, final_x = list(range(1, nx - 1)), nx - 1
     phase("c2_wait")
@@ -586,81 +598,77 @@
         b = other_x(k)
         send(wobuf.at[b, c], wobuf.at[b, c], WEIGHTS, wcr, c=sib)
 
-    phase("x3_wait")
-    outs, logs = [oxs[x, z]], [lxs[x]]
-    receive(oxr.at[pl.ds(0, nx * nz - 1)], x3r)
-    receive(lxr.at[pl.ds(0, nx * nz - 1)], x3lr)
-    for i, j in away:
-        if i or j:
-            at = other_x(i) * nz + other_z(j)
-            outs.append(oxr[at])
-            logs.append(lxr[at])
-    phase("combine")
-    picked = []
-    for v in logs:
-        row = v[0:1]
-        for g in range(1, kv):
-            row = jnp.where(my_g == g, v[g : g + 1], row)
-        picked.append(row)
-    weights = jnp.concatenate(picked, 0)
-    weights = jnp.exp(weights - jnp.max(weights, axis=0, keepdims=True))
-    wt[...] = as_columns(weights / jnp.sum(weights, axis=0, keepdims=True))
-    mine = wt[pl.ds(pl.multiple_of(my_quarter * ROWS, ROWS), ROWS), :]
-    attended = sum(mine[:, i : i + 1] * o.astype(F32) for i, o in enumerate(outs))
-    att[z] = attended.astype(BF16)
-
-    for k in z_far:
-        send(att.at[z], att.at[z], BIG, z4r, z=other_z(k))
-
-    phase("z4_wait")
+    phase("tail")
+    hear(hear_y.at[1], "y")
     receive(wobuf.at[:, sib], wcr)
-    receive(att.at[pl.ds(0, nz - 1)], z4r)
-
-    phase("w_out")
-    lhs = jnp.concatenate([att[t] for t in range(heads)], 1)
-    rhs = wobuf[...].reshape(nx * nc * HALF, heads * LANES)
-    got = lax.dot_general(lhs, rhs, (((1,), (1,)), ((), ())), preferred_element_type=F32)
-    low = iota((deep, LANES), 1) < HALF
-    for b in range(nx):
-        both = got[:, b * LANES : (b + 1) * LANES]
-        turned = pltpu.roll(both, HALF, 1)
-        p5s[b, 0] = jnp.where(low, both[0:deep], turned[deep:]).astype(BF16)
-        p5s[b, 1] = jnp.where(low, turned[0:deep], both[deep:]).astype(BF16)
-
-    me = c * ny + y
-    hear(hear_y.at[1], "y")
 
     def last(b, cc):
-        copy(p5s.at[b, cc], p5r.at[me], LAST, y5r, x=b, c=cc, y=x).start()
-
-    for k in x_far:
+        copy(p5s.at[b, cc], p5r.at[y], LAST, y5r, x=b, c=cc, y=x).start()
+
+    def finish():
+        sources = nx * nz
+        receive(oxr.at[pl.ds(0, 2 * sources - 1)], x3r)
+        receive(lxr.at[pl.ds(0, 2 * sources - 1)], x3lr)
+        shares = []
         for cc in range(nc):
-            last(other_x(k), cc)
-    last(x, sib)
-
-    @pl.when(x != y)
-    def _():
-        last(x, c)
-
-    @pl.when(x == y)
-    def _():
-        p5r[me] = p5s[x, c]
+            picked = []
+            for i in range(sources):
+                v = lxr[cc * sources + i]
+                row = v[0:1]
+                for g in range(1, kv):
+                    row = jnp.where(my_g == g, v[g : g + 1], row)
+                picked.append(row)
+            logs = jnp.concatenate(picked, 0)
+            logs = jnp.exp(logs - jnp.max(logs, axis=0, keepdims=True))
+            shares.append(logs / jnp.sum(logs, axis=0, keepdims=True))
+        wt[...] = as_columns(jnp.concatenate(shares, 0))
+        mine = wt[pl.ds(pl.multiple_of(my_quarter * ROWS, ROWS), ROWS), :]
+        for cc in range(nc):
+            span_of = range(cc * sources, (cc + 1) * sources)
+            attended = sum(mine[:, i : i + 1] * oxr[i].astype(F32) for i in span_of)
+            att[z, cc * ROWS : (cc + 1) * ROWS, :] = attended.astype(BF16)
+        for k in z_far:
+            copy(att.at[z], att.at[z], BIG, z4r, z=other_z(k)).start()
+        receive(att.at[pl.ds(0, nz - 1)], z4r)
+
+        lhs = jnp.concatenate([att[t] for t in range(heads)], 1)
+        rhs = wobuf[...].reshape(nx * nc * HALF, heads * LANES)
+        got = lax.dot_general(lhs, rhs, (((1,), (1,)), ((), ())), preferred_element_type=F32)
+        low = iota((ROWS, LANES), 1) < HALF
+        for b in range(nx):
+            both = got[:, b * LANES : (b + 1) * LANES]
+            turned = pltpu.roll(both, HALF, 1)
+            p5s[b, 0] = jnp.where(low, both[0:ROWS], turned[ROWS:]).astype(BF16)
+            p5s[b, 1] = jnp.where(low, turned[0:ROWS], both[ROWS:]).astype(BF16)
+        for k in x_far:
+            for cc in range(nc):
+                last(other_x(k), cc)
+        last(x, 0)
+
+        @pl.when(x != y)
+        def _():
+            last(x, 1)
+
+        @pl.when(x == y)
+        def _():
+            p5r[y] = p5s[x, 1]
+
+    pl.when(c == 1)(finish)
 
     phase("y5_wait")
-
-    @pl.when(x != y)
+    own_piece = jnp.logical_and(x == y, c == 1)
+
+    @pl.when(jnp.logical_not(own_piece))
     def _():
         receive(p5r, y5r)
 
-    @pl.when(x == y)
+    @pl.when(own_piece)
     def _():
-        receive(p5r.at[pl.ds(0, nc * ny - 1)], y5r)
-
-    for cc in range(nc):
-        final = sum(p5r[cc * ny + b].astype(F32) for b in range(ny))
-        at = cc * ROWS
-        out_ref[at : at + deep, :] = final[:, 0:HALF].astype(BF16)
-        out_ref[at + deep : at + ROWS, :] = pltpu.roll(final, HALF, 1)[:, 0:HALF].astype(BF16)
+        receive(p5r.at[pl.ds(0, ny - 1)], y5r)
+
+    final = sum(p5r[b].astype(F32) for b in range(ny))
+    out_ref[0:ROWS, :] = final[:, 0:HALF].astype(BF16)
+    out_ref[ROWS:, :] = pltpu.roll(final, HALF, 1)[:, 0:HALF].astype(BF16)
 
     phase("drain")
 
@@ -668,17 +676,27 @@
         copy(ref, ref, kind, c1r, c=sib).wait_send()
 
     line = LANES * jnp.dtype(BF16).itemsize
-    gone(dummy.at[pl.ds(0, sent[SMALL] // (2 * line))], SMALL)
-    gone(kraw.at[pl.ds(0, sent[BIG] // line)], BIG)
+    piece = ROWS * LANES * 2
+
+    @pl.when(c == 0)
+    def _():
+        gone(dummy.at[pl.ds(0, (sent[SMALL] + kv * LANES * 4) // (2 * line))], SMALL)
+        gone(kraw.at[pl.ds(0, (sent[BIG] + piece) // line)], BIG)
+
+    @pl.when(c == 1)
+    def _():
+        gone(dummy.at[pl.ds(0, sent[SMALL] // (2 * line))], SMALL)
+        gone(kraw.at[pl.ds(0, (sent[BIG] + (nz - 1) * nc * piece) // line)], BIG)
+
     gone(kraw.at[pl.ds(0, sent[WEIGHTS] // line)], WEIGHTS)
 
-    @pl.when(x != y)
+    @pl.when(jnp.logical_and(c == 1, x != y))
     def _():
-        gone(p5r, LAST)
-
-    @pl.when(x == y)
+        gone(kraw.at[pl.ds(0, nx * nc * piece // line)], LAST)
+
+    @pl.when(own_piece)
     def _():
-        gone(p5r.at[pl.ds(0, nc * ny - 1)], LAST)
+        gone(kraw.at[pl.ds(0, (nx * nc - 1) * piece // line)], LAST)
 
     phase(None)
 
@@ -719,11 +737,11 @@
         V((nc, nx, heads, ROWS, LANES), BF16), V((kv, rows, slots), F32),
         V((nx, block, LANES), F32), V((nx, kv, LANES), F32),
         V((nx, block, LANES), BF16), V((nx, block, LANES), BF16), V((nx, kv, LANES), F32), V((nx, kv, LANES), F32),
-        V((nx, nz, ROWS, LANES), BF16), V((nx * nz, ROWS, LANES), BF16),
-        V((nx, kv, LANES), F32), V((nx * nz, kv, LANES), F32),
+        V((nx, nz, ROWS, LANES), BF16), V((nc * nx * nz, ROWS, LANES), BF16),
+        V((nx, kv, LANES), F32), V((nc * nx * nz, kv, LANES), F32),
         V((LANES, LANES), F32),
-        V((heads, ROWS, LANES), BF16), V((nx, nc, HALF, w_out.shape[0]), BF16),
-        V((nx, nc, ROWS // 2, LANES), BF16), V((nc * ny, ROWS // 2, LANES), BF16),
+        V((heads, nc * ROWS, LANES), BF16), V((nx, nc, HALF, w_out.shape[0]), BF16),
+        V((nx, nc, ROWS, LANES), BF16), V((ny, ROWS, LANES), BF16),
         V((128, 1, LANES), F32), dma((11,)), dma((4,)),
         pltpu.SemaphoreType.REGULAR, pltpu.SemaphoreType.REGULAR((3,)), pltpu.SemaphoreType.REGULAR((2,)),
         V((ROWS // 2, cols), BF16), V((ROWS // 2, cols), BF16),

time: 57.3 us -> 56 us (0.977)
  Pallas kernels: 55.9 us -> 54.6 us
    pallas_call x1, Pallas kernels: 55.9 us -> 54.6 us  [local(): pl.pallas_call(functools.partial(kernel, (nx, nz, nc, ny, nx * nz * nc *...]
where the time goes in v6:
time: 56 us; the launch traced here: 55.9 us
  Pallas kernels  54.6 us (98%)
  between operations  0.66 us (1%)
  local copies, waits for them, and re-layouts  0.61 us (1%)
    pallas_call x1, Pallas kernels, local(): pl.pallas_call(functools.partial(kernel, (nx, nz, nc, ny, nx * nz * nc *...  54.6 us

profile of v6, /device:TPU:1, one launch (start us, length us, event | category | flops | bytes accessed | tf_op | source)
XLA Modules:
  0.0 55.9 jit_solution(11219041705255681752)
XLA Ops:
  0.7 54.6 %shard_map.109 = bf16[64,64]{1,0:T(8,128)(2,1)S(1)} custom-call(s32[64]{0:T(128)} %len_hbm.1, s32[1]{0:T(128)S(6)} %copy.14.start_hbm, bf16[64,256]{1,0:T(8,128)(2,1)} %bitcast.7, bf16[1,64]{1,0:T(2,128)(2,1)} %g_hbm.1, bf16[64,1024]{1,0:T(8,128)(2,1)} %wq_hbm.1, bf16[64,256]{1,0:T(8,128)(2,1)} %wk_hbm.1, bf16[64,256]{1,0:T(8,128)(2,1)} %wv_hbm.1, ...), custom_call_target="tpu_custom_call" | custom-call | tf_op jit(solution)/shard_map/pallas_call | solution.py:751
  55.3 0.6 %copy.13 = bf16[64,64]{1,0:T(8,128)(2,1)} copy(bf16[64,64]{1,0:T(8,128)(2,1)S(1)} %shard_map.109) | data formatting | bytes 16384

commit v7 on v6

--- a/solution.py
+++ b/solution.py
@@ -17,7 +17,7 @@
 HALF = 64
 ROWS = 32
 CHUNK = 128
-KEYS = 512
+KEYS = 1024
 SMALL, BIG, WEIGHTS, LAST = range(4)
 
 rope_base = 500000.0

time: 56 us -> 56 us (level)
  no operation moved by 1% of the time
where the time goes in v7:
time: 56 us; the launch traced here: 55.9 us
  Pallas kernels  54.6 us (98%)
  between operations  0.66 us (1%)
  local copies, waits for them, and re-layouts  0.61 us (1%)
    pallas_call x1, Pallas kernels, local(): pl.pallas_call(functools.partial(kernel, (nx, nz, nc, ny, nx * nz * nc *...  54.6 us

profile of v7, /device:TPU:1, one launch (start us, length us, event | category | flops | bytes accessed | tf_op | source)
XLA Modules:
  0.0 55.9 jit_solution(6221981906137811728)
XLA Ops:
  0.7 54.6 %shard_map.109 = bf16[64,64]{1,0:T(8,128)(2,1)S(1)} custom-call(s32[64]{0:T(128)} %len_hbm.1, s32[1]{0:T(128)S(6)} %copy.14.start_hbm, bf16[64,256]{1,0:T(8,128)(2,1)} %bitcast.7, bf16[1,64]{1,0:T(2,128)(2,1)} %g_hbm.1, bf16[64,1024]{1,0:T(8,128)(2,1)} %wq_hbm.1, bf16[64,256]{1,0:T(8,128)(2,1)} %wk_hbm.1, bf16[64,256]{1,0:T(8,128)(2,1)} %wv_hbm.1, ...), custom_call_target="tpu_custom_call" | custom-call | tf_op jit(solution)/shard_map/pallas_call | solution.py:751
  55.3 0.6 %copy.13 = bf16[64,64]{1,0:T(8,128)(2,1)} copy(bf16[64,64]{1,0:T(8,128)(2,1)S(1)} %shard_map.109) | data formatting | bytes 16384
